TPU v7x, 64 devices: a 2x2x8 block of a 4x4x8 slice. The times are simulated.
64 devices in a mesh: dp: 4 (over x, y), cp: 16 (over z, core).
Axes of the slice: x: 2, y: 2, z: 8, core: 2. Of those that a mesh axis runs over, the one named last changes fastest.
The devices are a block of a 4x4x8 slice.
Arguments:
- tokens: bfloat16 [8, 3072, 2048], P('dp', 'cp'), parts along dimension 0
- positions: int32 [8, 3072], P('dp', 'cp'), parts along dimension 0
- norm_gain: float32 [2048], replicated
- w_query: bfloat16 [2048, 2048], replicated
- w_key: bfloat16 [2048, 256], replicated
- w_value: bfloat16 [2048, 256], replicated
- w_out: bfloat16 [2048, 2048], replicated
- d_out: bfloat16 [8, 3072, 2048], P('dp', 'cp'), parts along dimension 0
Outputs:
- output 1: bfloat16 [8, 3072, 2048], P('dp', 'cp'), parts along dimension 0
- output 2: bfloat16 [8, 3072, 2048], P('dp', 'cp'), parts along dimension 0
- output 3: float32 [8192, 2048], P('dp'), parts along dimension 0
- output 4: float32 [8192, 256], P('dp'), parts along dimension 0
- output 5: float32 [8192, 256], P('dp'), parts along dimension 0
- output 6: float32 [8192, 2048], P('dp'), parts along dimension 0
- output 7: float32 [8192], P('dp'), parts along dimension 0
There are 4 independent parts. A program takes and returns all parts, laid end to end along the dimension named above; an argument that names none is the same for every part.
All inputs are finite; a program needn't handle non-finite values.
Results may differ from a plain program's by a relative error of at most 0.012375.
Values are sent between devices in bfloat16 or wider.
A program may use at most 768 MiB of HBM per device.

v0:
```python
import jax
import jax.numpy as jnp
from jax import lax
from jax.sharding import PartitionSpec as P, NamedSharding

NORM_EPS = 1e-6
ROPE_BASE = 10000.0
NEG_BIG = -1e30


def layer_norm(tokens, norm_gain):
    x_float = tokens.astype(jnp.float32)
    centered = x_float - jnp.mean(x_float, axis=-1, keepdims=True)
    inv_std = lax.rsqrt(jnp.mean(centered * centered, axis=-1, keepdims=True) + NORM_EPS)
    x_hat = centered * inv_std
    return (x_hat * norm_gain).astype(jnp.bfloat16), x_hat, inv_std


def layer_norm_grad(d_h, x_hat, inv_std, norm_gain):
    d_hat = d_h * norm_gain
    mean_d = jnp.mean(d_hat, axis=-1, keepdims=True)
    mean_dx = jnp.mean(d_hat * x_hat, axis=-1, keepdims=True)
    return inv_std * (d_hat - mean_d - x_hat * mean_dx)


def rope_tables(positions, head_dim):
    half_dim = head_dim // 2
    inv_freq = ROPE_BASE ** (-(jnp.arange(half_dim, dtype=jnp.float32) * (2.0 / head_dim)))
    angles = positions.astype(jnp.float32)[..., None] * inv_freq
    return jnp.cos(angles), jnp.sin(angles)


def rotate(values, cos_t, sin_t):
    half_dim = values.shape[-1] // 2
    front_half, back_half = values[..., :half_dim], values[..., half_dim:]
    return jnp.concatenate([front_half * cos_t - back_half * sin_t, back_half * cos_t + front_half * sin_t], axis=-1)


def rotate_back(grad_vals, cos_t, sin_t):
    half_dim = grad_vals.shape[-1] // 2
    front_half, back_half = grad_vals[..., :half_dim], grad_vals[..., half_dim:]
    return jnp.concatenate([front_half * cos_t + back_half * sin_t, back_half * cos_t - front_half * sin_t], axis=-1)


def attend_block(run_max, run_sum, run_acc, q_blk, k_blk, v_blk, key_mask):
    score_scale = q_blk.shape[-1] ** -0.5
    scores = jnp.einsum('crie,cle->cril', q_blk, k_blk, preferred_element_type=jnp.float32) * score_scale
    if key_mask is not None:
        scores = jnp.where(key_mask, scores, NEG_BIG)
    new_max = jnp.maximum(run_max, jnp.max(scores, axis=-1))
    exp_scores = jnp.exp(scores - new_max[..., None])
    rescale = jnp.exp(run_max - new_max)
    new_sum = rescale * run_sum + jnp.sum(exp_scores, axis=-1)
    new_acc = rescale[..., None] * run_acc + jnp.einsum('cril,cle->crie', exp_scores.astype(jnp.bfloat16), v_blk, preferred_element_type=jnp.float32)
    return new_max, new_sum, new_acc


def attend_grad(q_blk, da_blk, lse_blk, delta_blk, k_blk, v_blk, key_mask):
    score_scale = q_blk.shape[-1] ** -0.5
    scores = jnp.einsum('crie,cle->cril', q_blk, k_blk, preferred_element_type=jnp.float32) * score_scale
    if key_mask is not None:
        scores = jnp.where(key_mask, scores, NEG_BIG)
    attn_p = jnp.exp(scores - lse_blk[..., None])
    d_probs = jnp.einsum('crie,cle->cril', da_blk, v_blk, preferred_element_type=jnp.float32)
    d_scores = (attn_p * (d_probs - delta_blk[..., None])).astype(jnp.bfloat16)
    dq_part = jnp.einsum('cril,cle->crie', d_scores, k_blk, preferred_element_type=jnp.float32) * score_scale
    dk_part = jnp.einsum('cril,crie->cle', d_scores, q_blk, preferred_element_type=jnp.float32) * score_scale
    dv_part = jnp.einsum('cril,crie->cle', attn_p.astype(jnp.bfloat16), da_blk, preferred_element_type=jnp.float32)
    return dq_part, dk_part, dv_part


def solution(mesh):
    cp_size = mesh.shape['cp']
    next_perm = [(src, (src + 1) % cp_size) for src in range(cp_size)]

    def send_next(tree_vals):
        return lax.ppermute(tree_vals, 'cp', next_perm)

    def local_fn(tokens, positions, norm_gain, w_query, w_key, w_value, w_out, d_out):
        n_seq, blk_len, model_dim = tokens.shape
        head_dim = w_key.shape[1]
        num_heads = w_query.shape[1] // head_dim
        q_width = num_heads * head_dim
        half_len = blk_len // 2
        my_index = lax.axis_index('cp')
        h_norm, x_hat, inv_std = layer_norm(tokens, norm_gain)
        cos_t, sin_t = rope_tables(positions, head_dim)
        cos_h, sin_h = cos_t[:, :, None, :], sin_t[:, :, None, :]
        q_lin = jnp.einsum('bld,dn->bln', h_norm, w_query, preferred_element_type=jnp.float32)
        q_rot = rotate(q_lin.reshape(n_seq, blk_len, num_heads, head_dim), cos_h, sin_h).astype(jnp.bfloat16)
        k_rot = rotate(jnp.einsum('bld,dc->blc', h_norm, w_key, preferred_element_type=jnp.float32), cos_t, sin_t).astype(jnp.bfloat16)
        v_proj = jnp.einsum('bld,dc->blc', h_norm, w_value, preferred_element_type=jnp.float32).astype(jnp.bfloat16)
        key_mask = positions[:, None, None, :] <= positions[:, :, None, None]

        init_max = jnp.full((n_seq, blk_len, num_heads), NEG_BIG, jnp.float32)
        init_sum = jnp.zeros((n_seq, blk_len, num_heads), jnp.float32)
        init_acc = jnp.zeros((n_seq, blk_len, num_heads, head_dim), jnp.float32)
        run_stats = attend_block(init_max, init_sum, init_acc, q_rot, k_rot, v_proj, key_mask)

        def from_before(k_blk, v_blk, max_in, sum_in, acc_in):
            return attend_block(max_in, sum_in, acc_in, q_rot, k_blk[:, :half_len], v_blk[:, :half_len], None)

        def from_after(k_blk, v_blk, max_in, sum_in, acc_in):
            new_max, new_sum, new_acc = attend_block(max_in[:, half_len:], sum_in[:, half_len:], acc_in[:, half_len:], q_rot[:, half_len:], k_blk, v_blk, None)
            return (jnp.concatenate([max_in[:, :half_len], new_max], axis=1),
                    jnp.concatenate([sum_in[:, :half_len], new_sum], axis=1),
                    jnp.concatenate([acc_in[:, :half_len], new_acc], axis=1))

        def fwd_step(step_idx, loop_state):
            k_cur, v_cur, run_max, run_sum, run_acc = loop_state
            k_cur, v_cur = send_next((k_cur, v_cur))
            src_index = (my_index - step_idx) % cp_size
            run_max, run_sum, run_acc = lax.cond(src_index < my_index, from_before, from_after, k_cur, v_cur, run_max, run_sum, run_acc)
            return k_cur, v_cur, run_max, run_sum, run_acc

        loop_state = lax.fori_loop(1, cp_size, fwd_step, (k_rot, v_proj) + run_stats)
        run_max, run_sum, run_acc = loop_state[2], loop_state[3], loop_state[4]
        attn_out = (run_acc / run_sum[..., None]).astype(jnp.bfloat16)
        log_sum = run_max + jnp.log(run_sum)
        attn_flat = attn_out.reshape(n_seq, blk_len, q_width)
        o_proj = jnp.einsum('bln,nd->bld', attn_flat, w_out, preferred_element_type=jnp.float32).astype(jnp.bfloat16)
        out_y = (tokens.astype(jnp.float32) + o_proj.astype(jnp.float32)).astype(jnp.bfloat16)

        d_attn = jnp.einsum('bld,nd->bln', d_out, w_out, preferred_element_type=jnp.float32).astype(jnp.bfloat16).reshape(n_seq, blk_len, num_heads, head_dim)
        grad_wo = jnp.einsum('bln,bld->nd', attn_flat, d_out, preferred_element_type=jnp.float32)
        out_delta = jnp.sum(d_attn.astype(jnp.float32) * attn_out.astype(jnp.float32), axis=-1)
        dq_acc, dk_acc, dv_acc = attend_grad(q_rot, d_attn, log_sum, out_delta, k_rot, v_proj, key_mask)

        def grad_before(k_blk, v_blk, dk_in, dv_in, dq_in):
            dq_part, dk_part, dv_part = attend_grad(q_rot, d_attn, log_sum, out_delta, k_blk[:, :half_len], v_blk[:, :half_len], None)
            dk_new = jnp.concatenate([dk_in[:, :half_len] + dk_part, dk_in[:, half_len:]], axis=1)
            dv_new = jnp.concatenate([dv_in[:, :half_len] + dv_part, dv_in[:, half_len:]], axis=1)
            return dk_new, dv_new, dq_in + dq_part

        def grad_after(k_blk, v_blk, dk_in, dv_in, dq_in):
            dq_part, dk_part, dv_part = attend_grad(q_rot[:, half_len:], d_attn[:, half_len:], log_sum[:, half_len:], out_delta[:, half_len:], k_blk, v_blk, None)
            dq_new = jnp.concatenate([dq_in[:, :half_len], dq_in[:, half_len:] + dq_part], axis=1)
            return dk_in + dk_part, dv_in + dv_part, dq_new

        def bwd_step(step_idx, loop_state):
            k_cur, v_cur, dk_cur, dv_cur, dq_cur = loop_state
            k_cur, v_cur, dk_cur, dv_cur = send_next((k_cur, v_cur, dk_cur, dv_cur))
            src_index = (my_index - step_idx) % cp_size
            dk_cur, dv_cur, dq_cur = lax.cond(src_index < my_index, grad_before, grad_after, k_cur, v_cur, dk_cur, dv_cur, dq_cur)
            return k_cur, v_cur, dk_cur, dv_cur, dq_cur

        loop_state = lax.fori_loop(1, cp_size, bwd_step, (k_rot, v_proj, dk_acc, dv_acc, dq_acc))
        dk_home, dv_home = send_next((loop_state[2], loop_state[3]))
        dq_acc = loop_state[4]

        dq_pre = rotate_back(dq_acc, cos_h, sin_h).astype(jnp.bfloat16).reshape(n_seq, blk_len, q_width)
        dk_pre = rotate_back(dk_home, cos_t, sin_t).astype(jnp.bfloat16)
        dv_pre = dv_home.astype(jnp.bfloat16)
        grad_wq = jnp.einsum('bld,bln->dn', h_norm, dq_pre, preferred_element_type=jnp.float32)
        grad_wk = jnp.einsum('bld,blc->dc', h_norm, dk_pre, preferred_element_type=jnp.float32)
        grad_wv = jnp.einsum('bld,blc->dc', h_norm, dv_pre, preferred_element_type=jnp.float32)
        d_h = (jnp.einsum('bln,dn->bld', dq_pre, w_query, preferred_element_type=jnp.float32)
               + jnp.einsum('blc,dc->bld', dk_pre, w_key, preferred_element_type=jnp.float32)
               + jnp.einsum('blc,dc->bld', dv_pre, w_value, preferred_element_type=jnp.float32))
        grad_x = (d_out.astype(jnp.float32) + layer_norm_grad(d_h, x_hat, inv_std, norm_gain)).astype(jnp.bfloat16)
        grad_gain = jnp.sum(d_h * x_hat, axis=(0, 1))
        grad_wq, grad_wk, grad_wv, grad_wo, grad_gain = lax.psum((grad_wq, grad_wk, grad_wv, grad_wo, grad_gain), 'cp')
        return out_y, grad_x, grad_wq, grad_wk, grad_wv, grad_wo, grad_gain

    seq_spec = P('dp', 'cp', None)
    rep_spec = P(None, None)
    part_spec = P('dp', None)
    return jax.shard_map(local_fn, mesh=mesh,
                         in_specs=(seq_spec, P('dp', 'cp'), P(None), rep_spec, rep_spec, rep_spec, rep_spec, seq_spec),
                         out_specs=(seq_spec, seq_spec, part_spec, part_spec, part_spec, part_spec, P('dp')),
                         check_vma=False)
```

profile of v0, /device:TPU:21, one launch (start us, length us, event | category | flops | bytes accessed | tf_op | source)
XLA Modules:
  0.0 1234.8 jit_solution(13759901210068657295)
XLA Ops:
  35.3 243.5 %while.46 = (s32[]{:T(128)}, bf16[2,192,256]{2,1,0:T(8,128)(2,1)S(1)}, bf16[2,192,256]{2,1,0:T(8,128)(2,1)S(1)}, f32[2,192,8]{1,2,0:T(8,128)S(1)}, f32[2,192,8]{...) while((s32[]{:T(128)}, ...), condition=%wide.region_11.12_spmd, body=%wide.region_4.11_spmd.sunk | while | flops 305341440 | bytes 33239520 | solution.py:116
  43.6 9.5 conditional.4
  60.4 7.1 conditional.4
  77.2 7.1 conditional.4
  91.6 7.1 conditional.4
  106.0 7.1 conditional.4
  122.8 7.1 conditional.4
  139.7 7.1 conditional.4
  155.3 7.1 conditional.4
  165.0 5.7 collective-permute-start
  173.3 7.1 conditional.4
  182.9 5.7 collective-permute-start
  191.3 7.1 conditional.4
  206.9 7.1 conditional.4
  216.6 5.7 collective-permute-start
  224.9 7.1 conditional.4
  240.5 7.1 conditional.4
  256.1 7.1 conditional.4
  271.7 7.1 conditional.4
  278.9 7.3 fusion.70
  301.2 440.2 %while.47 = (s32[]{:T(128)}, bf16[2,192,256]{2,1,0:T(8,128)(2,1)}, bf16[2,192,256]{2,1,0:T(8,128)(2,1)}, f32[2,192,256]{2,1,0:T(8,128)}, f32[2,192,256]{2,1,0:T(...) while((s32[]{:T(128)}, bf16[2,192,256]{2,1,0:T(8,128)(2,1)}, ...), condition=%wide.region_16.17_spmd, body=%wide.region_13.16_spmd.sunk | while | flops 758661120 | bytes 59278000 | solution.py:147
  317.7 12.8 %conditional.5 = (f32[2,192,256]{2,1,0:T(8,128)}, f32[2,192,256]{2,1,0:T(8,128)}, f32[2,192,8,256]{3,2,1,0:T(8,128)}) conditional(s32[]{:T(128)} %convert_element_type.198, (bf16[2,192,8,256]{3,1,2,0:T(8,128)(2,1)}, bf16[2,192,256]{2,1,0:T(8,128)(2,1)S(1)}, f32[2,192,8]{2,1,0:T(8,128)S(1)}, bf16[2,192,8,256]{3,1,2,0:T(8,128)(2,1)S(1)}, ...), branch_computations={%region_14.14_spmd, %region_15.15_spmd} | conditional | flops 758661120 | bytes 53772396 | solution.py:144
  346.8 11.4 conditional.5
  375.9 11.4 conditional.5
  389.7 5.7 collective-permute-start.4
  405.1 11.4 conditional.5
  435.3 11.4 conditional.5
  465.6 11.4 conditional.5
  494.5 11.4 conditional.5
  508.4 6.8 collective-permute-start.4
  524.8 11.4 conditional.5
  538.7 6.8 collective-permute-start.4
  555.1 11.4 conditional.5
  584.9 11.4 conditional.5
  598.8 5.9 collective-permute-start.4
  614.3 11.4 conditional.5
  643.2 11.4 conditional.5
  672.1 11.4 conditional.5
  701.1 11.4 conditional.5
  730.0 11.4 conditional.5
  761.7 10.5 convolution_bitcast_fusion.5
  772.1 8.5 convolution_bitcast_fusion.4
  786.2 6.5 fusion.48
  792.7 8.2 fusion.66
  804.8 32.8 %psum.39 = f32[2048]{0:T(1024)} all-reduce(f32[2048]{0:T(1024)S(1)} %get-tuple-element.727), channel_id=1, replica_groups=mesh['dp'=4,'cp'=16] {'cp'}, use_global_device_ids=true, to_apply=%region_24.25 | all-reduce | flops 2048 | bytes 16384 | tf_op jit(solution)/shard_map/psum | solution.py:162
  842.4 360.0 %all-reduce.3.cloned.1.call-done = (f32[2048,2048]{1,0:T(8,128)}, f32[2048,256]{1,0:T(8,128)}, f32[2048,256]{1,0:T(8,128)}, f32[2048,2048]{1,0:T(8,128)}) async-done(((f32[2048,2048]{1,0:T(8,128)}, f32[2048,256]{1,0:T(8,128)}, f32[2048,256]{1,0:T(8,128)}, f32[2048,2048]{1,0:T(8,128)}), (f32[2048,2048]{1,0:T(8,128)}, f32[2048,256]{1,0:T(8,128)}, f32[2048,256]{1,0:T(8,128)}, ...) | async-done | bytes 37748752 | tf_op jit(solution)/shard_map/psum | solution.py:162
  1202.3 14.1 %copy.191 = f32[2048,2048]{1,0:T(8,128)} copy(f32[2048,2048]{1,0:T(8,128)} %get-tuple-element.1032) | data formatting | bytes 33554432
  1221.3 6.2 copy.194
  (802 shorter events, 720.4 us)
Async XLA Ops:
  7.2 1195.1 %all-reduce.3.cloned.1.call-start = ((), (), s32[]{:S(2)}) async-start(), calls=%async_computation | async-start | bytes 75497472 | tf_op jit(solution)/shard_map/psum | solution.py:162
  67.5 7.6 collective-permute-start.1
  162.4 8.3 collective-permute-start.1
  165.0 8.3 collective-permute-start
  180.4 8.3 collective-permute-start.1
  182.9 8.3 collective-permute-start
  214.0 8.3 collective-permute-start.1
  216.6 8.3 collective-permute-start
  263.2 7.3 collective-permute-start.1
  301.4 16.4 %collective-permute-start.5 = (f32[2,192,256]{2,1,0:T(8,128)}, f32[2,192,256]{2,1,0:T(8,128)}, u32[]{:S(2)}, u32[]{:S(2)}) collective-permute-start(f32[2,192,256]{2,1,0:T(8,128)} %get-tuple-element.1004), channel_id=1, source_target_pairs={{0,1},{1,2},{2,3},{3,4},{4,5},{5,6},{6,7},{7,8},{8,9},{9,10},{10,1... | collective-permute-start | bytes 1179656 | tf_op jit(solution)/shard_map/while/body/eval_jaxpr/ppermute | solution.py:77
  303.9 13.8 %collective-permute-start.4 = (f32[2,192,256]{2,1,0:T(8,128)}, f32[2,192,256]{2,1,0:T(8,128)}, u32[]{:S(2)}, u32[]{:S(2)}) collective-permute-start(f32[2,192,256]{2,1,0:T(8,128)} %get-tuple-element.1003), channel_id=1, source_target_pairs={{0,1},{1,2},{2,3},{3,4},{4,5},{5,6},{6,7},{7,8},{8,9},{9,10},{10,1... | collective-permute-start | bytes 1179656 | tf_op jit(solution)/shard_map/while/body/eval_jaxpr/ppermute | solution.py:77
  307.2 7.7 collective-permute-start.3
  309.7 7.3 collective-permute-start.2
  330.5 16.3 %collective-permute-start.5 = (f32[2,192,256]{2,1,0:T(8,128)}, f32[2,192,256]{2,1,0:T(8,128)}, u32[]{:S(2)}, u32[]{:S(2)}) collective-permute-start(f32[2,192,256]{2,1,0:T(8,128)} %get-tuple-element.1004), channel_id=1, source_target_pairs={{0,1},{1,2},{2,3},{3,4},{4,5},{5,6},{6,7},{7,8},{8,9},{9,10},{10,1... | collective-permute-start | bytes 1179656 | tf_op jit(solution)/shard_map/while/body/eval_jaxpr/ppermute | solution.py:77
  333.0 13.8 %collective-permute-start.4 = (f32[2,192,256]{2,1,0:T(8,128)}, f32[2,192,256]{2,1,0:T(8,128)}, u32[]{:S(2)}, u32[]{:S(2)}) collective-permute-start(f32[2,192,256]{2,1,0:T(8,128)} %get-tuple-element.1003), channel_id=1, source_target_pairs={{0,1},{1,2},{2,3},{3,4},{4,5},{5,6},{6,7},{7,8},{8,9},{9,10},{10,1... | collective-permute-start | bytes 1179656 | tf_op jit(solution)/shard_map/while/body/eval_jaxpr/ppermute | solution.py:77
  336.3 7.7 collective-permute-start.3
  358.2 17.7 %collective-permute-start.5 = (f32[2,192,256]{2,1,0:T(8,128)}, f32[2,192,256]{2,1,0:T(8,128)}, u32[]{:S(2)}, u32[]{:S(2)}) collective-permute-start(f32[2,192,256]{2,1,0:T(8,128)} %get-tuple-element.1004), channel_id=1, source_target_pairs={{0,1},{1,2},{2,3},{3,4},{4,5},{5,6},{6,7},{7,8},{8,9},{9,10},{10,1... | collective-permute-start | bytes 1179656 | tf_op jit(solution)/shard_map/while/body/eval_jaxpr/ppermute | solution.py:77
  362.0 13.8 %collective-permute-start.4 = (f32[2,192,256]{2,1,0:T(8,128)}, f32[2,192,256]{2,1,0:T(8,128)}, u32[]{:S(2)}, u32[]{:S(2)}) collective-permute-start(f32[2,192,256]{2,1,0:T(8,128)} %get-tuple-element.1003), channel_id=1, source_target_pairs={{0,1},{1,2},{2,3},{3,4},{4,5},{5,6},{6,7},{7,8},{8,9},{9,10},{10,1... | collective-permute-start | bytes 1179656 | tf_op jit(solution)/shard_map/while/body/eval_jaxpr/ppermute | solution.py:77
  365.4 7.7 collective-permute-start.3
  387.2 17.8 %collective-permute-start.5 = (f32[2,192,256]{2,1,0:T(8,128)}, f32[2,192,256]{2,1,0:T(8,128)}, u32[]{:S(2)}, u32[]{:S(2)}) collective-permute-start(f32[2,192,256]{2,1,0:T(8,128)} %get-tuple-element.1004), channel_id=1, source_target_pairs={{0,1},{1,2},{2,3},{3,4},{4,5},{5,6},{6,7},{7,8},{8,9},{9,10},{10,1... | collective-permute-start | bytes 1179656 | tf_op jit(solution)/shard_map/while/body/eval_jaxpr/ppermute | solution.py:77
  389.7 15.3 %collective-permute-start.4 = (f32[2,192,256]{2,1,0:T(8,128)}, f32[2,192,256]{2,1,0:T(8,128)}, u32[]{:S(2)}, u32[]{:S(2)}) collective-permute-start(f32[2,192,256]{2,1,0:T(8,128)} %get-tuple-element.1003), channel_id=1, source_target_pairs={{0,1},{1,2},{2,3},{3,4},{4,5},{5,6},{6,7},{7,8},{8,9},{9,10},{10,1... | collective-permute-start | bytes 1179656 | tf_op jit(solution)/shard_map/while/body/eval_jaxpr/ppermute | solution.py:77
  416.5 18.9 %collective-permute-start.5 = (f32[2,192,256]{2,1,0:T(8,128)}, f32[2,192,256]{2,1,0:T(8,128)}, u32[]{:S(2)}, u32[]{:S(2)}) collective-permute-start(f32[2,192,256]{2,1,0:T(8,128)} %get-tuple-element.1004), channel_id=1, source_target_pairs={{0,1},{1,2},{2,3},{3,4},{4,5},{5,6},{6,7},{7,8},{8,9},{9,10},{10,1... | collective-permute-start | bytes 1179656 | tf_op jit(solution)/shard_map/while/body/eval_jaxpr/ppermute | solution.py:77
  419.0 16.4 %collective-permute-start.4 = (f32[2,192,256]{2,1,0:T(8,128)}, f32[2,192,256]{2,1,0:T(8,128)}, u32[]{:S(2)}, u32[]{:S(2)}) collective-permute-start(f32[2,192,256]{2,1,0:T(8,128)} %get-tuple-element.1003), channel_id=1, source_target_pairs={{0,1},{1,2},{2,3},{3,4},{4,5},{5,6},{6,7},{7,8},{8,9},{9,10},{10,1... | collective-permute-start | bytes 1179656 | tf_op jit(solution)/shard_map/while/body/eval_jaxpr/ppermute | solution.py:77
  424.4 7.7 collective-permute-start.3
  446.7 18.9 %collective-permute-start.5 = (f32[2,192,256]{2,1,0:T(8,128)}, f32[2,192,256]{2,1,0:T(8,128)}, u32[]{:S(2)}, u32[]{:S(2)}) collective-permute-start(f32[2,192,256]{2,1,0:T(8,128)} %get-tuple-element.1004), channel_id=1, source_target_pairs={{0,1},{1,2},{2,3},{3,4},{4,5},{5,6},{6,7},{7,8},{8,9},{9,10},{10,1... | collective-permute-start | bytes 1179656 | tf_op jit(solution)/shard_map/while/body/eval_jaxpr/ppermute | solution.py:77
  449.2 16.4 %collective-permute-start.4 = (f32[2,192,256]{2,1,0:T(8,128)}, f32[2,192,256]{2,1,0:T(8,128)}, u32[]{:S(2)}, u32[]{:S(2)}) collective-permute-start(f32[2,192,256]{2,1,0:T(8,128)} %get-tuple-element.1003), channel_id=1, source_target_pairs={{0,1},{1,2},{2,3},{3,4},{4,5},{5,6},{6,7},{7,8},{8,9},{9,10},{10,1... | collective-permute-start | bytes 1179656 | tf_op jit(solution)/shard_map/while/body/eval_jaxpr/ppermute | solution.py:77
  454.7 7.7 collective-permute-start.3
  457.2 7.8 collective-permute-start.2
  477.0 17.5 %collective-permute-start.5 = (f32[2,192,256]{2,1,0:T(8,128)}, f32[2,192,256]{2,1,0:T(8,128)}, u32[]{:S(2)}, u32[]{:S(2)}) collective-permute-start(f32[2,192,256]{2,1,0:T(8,128)} %get-tuple-element.1004), channel_id=1, source_target_pairs={{0,1},{1,2},{2,3},{3,4},{4,5},{5,6},{6,7},{7,8},{8,9},{9,10},{10,1... | collective-permute-start | bytes 1179656 | tf_op jit(solution)/shard_map/while/body/eval_jaxpr/ppermute | solution.py:77
  479.5 15.0 %collective-permute-start.4 = (f32[2,192,256]{2,1,0:T(8,128)}, f32[2,192,256]{2,1,0:T(8,128)}, u32[]{:S(2)}, u32[]{:S(2)}) collective-permute-start(f32[2,192,256]{2,1,0:T(8,128)} %get-tuple-element.1003), channel_id=1, source_target_pairs={{0,1},{1,2},{2,3},{3,4},{4,5},{5,6},{6,7},{7,8},{8,9},{9,10},{10,1... | collective-permute-start | bytes 1179656 | tf_op jit(solution)/shard_map/while/body/eval_jaxpr/ppermute | solution.py:77
  505.9 18.9 %collective-permute-start.5 = (f32[2,192,256]{2,1,0:T(8,128)}, f32[2,192,256]{2,1,0:T(8,128)}, u32[]{:S(2)}, u32[]{:S(2)}) collective-permute-start(f32[2,192,256]{2,1,0:T(8,128)} %get-tuple-element.1004), channel_id=1, source_target_pairs={{0,1},{1,2},{2,3},{3,4},{4,5},{5,6},{6,7},{7,8},{8,9},{9,10},{10,1... | collective-permute-start | bytes 1179656 | tf_op jit(solution)/shard_map/while/body/eval_jaxpr/ppermute | solution.py:77
  508.4 16.4 %collective-permute-start.4 = (f32[2,192,256]{2,1,0:T(8,128)}, f32[2,192,256]{2,1,0:T(8,128)}, u32[]{:S(2)}, u32[]{:S(2)}) collective-permute-start(f32[2,192,256]{2,1,0:T(8,128)} %get-tuple-element.1003), channel_id=1, source_target_pairs={{0,1},{1,2},{2,3},{3,4},{4,5},{5,6},{6,7},{7,8},{8,9},{9,10},{10,1... | collective-permute-start | bytes 1179656 | tf_op jit(solution)/shard_map/while/body/eval_jaxpr/ppermute | solution.py:77
  536.2 18.9 %collective-permute-start.5 = (f32[2,192,256]{2,1,0:T(8,128)}, f32[2,192,256]{2,1,0:T(8,128)}, u32[]{:S(2)}, u32[]{:S(2)}) collective-permute-start(f32[2,192,256]{2,1,0:T(8,128)} %get-tuple-element.1004), channel_id=1, source_target_pairs={{0,1},{1,2},{2,3},{3,4},{4,5},{5,6},{6,7},{7,8},{8,9},{9,10},{10,1... | collective-permute-start | bytes 1179656 | tf_op jit(solution)/shard_map/while/body/eval_jaxpr/ppermute | solution.py:77
  538.7 16.4 %collective-permute-start.4 = (f32[2,192,256]{2,1,0:T(8,128)}, f32[2,192,256]{2,1,0:T(8,128)}, u32[]{:S(2)}, u32[]{:S(2)}) collective-permute-start(f32[2,192,256]{2,1,0:T(8,128)} %get-tuple-element.1003), channel_id=1, source_target_pairs={{0,1},{1,2},{2,3},{3,4},{4,5},{5,6},{6,7},{7,8},{8,9},{9,10},{10,1... | collective-permute-start | bytes 1179656 | tf_op jit(solution)/shard_map/while/body/eval_jaxpr/ppermute | solution.py:77
  566.5 18.4 %collective-permute-start.5 = (f32[2,192,256]{2,1,0:T(8,128)}, f32[2,192,256]{2,1,0:T(8,128)}, u32[]{:S(2)}, u32[]{:S(2)}) collective-permute-start(f32[2,192,256]{2,1,0:T(8,128)} %get-tuple-element.1004), channel_id=1, source_target_pairs={{0,1},{1,2},{2,3},{3,4},{4,5},{5,6},{6,7},{7,8},{8,9},{9,10},{10,1... | collective-permute-start | bytes 1179656 | tf_op jit(solution)/shard_map/while/body/eval_jaxpr/ppermute | solution.py:77
  569.0 15.9 %collective-permute-start.4 = (f32[2,192,256]{2,1,0:T(8,128)}, f32[2,192,256]{2,1,0:T(8,128)}, u32[]{:S(2)}, u32[]{:S(2)}) collective-permute-start(f32[2,192,256]{2,1,0:T(8,128)} %get-tuple-element.1003), channel_id=1, source_target_pairs={{0,1},{1,2},{2,3},{3,4},{4,5},{5,6},{6,7},{7,8},{8,9},{9,10},{10,1... | collective-permute-start | bytes 1179656 | tf_op jit(solution)/shard_map/while/body/eval_jaxpr/ppermute | solution.py:77
  596.2 18.0 %collective-permute-start.5 = (f32[2,192,256]{2,1,0:T(8,128)}, f32[2,192,256]{2,1,0:T(8,128)}, u32[]{:S(2)}, u32[]{:S(2)}) collective-permute-start(f32[2,192,256]{2,1,0:T(8,128)} %get-tuple-element.1004), channel_id=1, source_target_pairs={{0,1},{1,2},{2,3},{3,4},{4,5},{5,6},{6,7},{7,8},{8,9},{9,10},{10,1... | collective-permute-start | bytes 1179656 | tf_op jit(solution)/shard_map/while/body/eval_jaxpr/ppermute | solution.py:77
  598.8 15.5 %collective-permute-start.4 = (f32[2,192,256]{2,1,0:T(8,128)}, f32[2,192,256]{2,1,0:T(8,128)}, u32[]{:S(2)}, u32[]{:S(2)}) collective-permute-start(f32[2,192,256]{2,1,0:T(8,128)} %get-tuple-element.1003), channel_id=1, source_target_pairs={{0,1},{1,2},{2,3},{3,4},{4,5},{5,6},{6,7},{7,8},{8,9},{9,10},{10,1... | collective-permute-start | bytes 1179656 | tf_op jit(solution)/shard_map/while/body/eval_jaxpr/ppermute | solution.py:77
  625.7 17.5 %collective-permute-start.5 = (f32[2,192,256]{2,1,0:T(8,128)}, f32[2,192,256]{2,1,0:T(8,128)}, u32[]{:S(2)}, u32[]{:S(2)}) collective-permute-start(f32[2,192,256]{2,1,0:T(8,128)} %get-tuple-element.1004), channel_id=1, source_target_pairs={{0,1},{1,2},{2,3},{3,4},{4,5},{5,6},{6,7},{7,8},{8,9},{9,10},{10,1... | collective-permute-start | bytes 1179656 | tf_op jit(solution)/shard_map/while/body/eval_jaxpr/ppermute | solution.py:77
  628.2 15.0 %collective-permute-start.4 = (f32[2,192,256]{2,1,0:T(8,128)}, f32[2,192,256]{2,1,0:T(8,128)}, u32[]{:S(2)}, u32[]{:S(2)}) collective-permute-start(f32[2,192,256]{2,1,0:T(8,128)} %get-tuple-element.1003), channel_id=1, source_target_pairs={{0,1},{1,2},{2,3},{3,4},{4,5},{5,6},{6,7},{7,8},{8,9},{9,10},{10,1... | collective-permute-start | bytes 1179656 | tf_op jit(solution)/shard_map/while/body/eval_jaxpr/ppermute | solution.py:77
  654.6 17.5 %collective-permute-start.5 = (f32[2,192,256]{2,1,0:T(8,128)}, f32[2,192,256]{2,1,0:T(8,128)}, u32[]{:S(2)}, u32[]{:S(2)}) collective-permute-start(f32[2,192,256]{2,1,0:T(8,128)} %get-tuple-element.1004), channel_id=1, source_target_pairs={{0,1},{1,2},{2,3},{3,4},{4,5},{5,6},{6,7},{7,8},{8,9},{9,10},{10,1... | collective-permute-start | bytes 1179656 | tf_op jit(solution)/shard_map/while/body/eval_jaxpr/ppermute | solution.py:77
  657.1 15.0 %collective-permute-start.4 = (f32[2,192,256]{2,1,0:T(8,128)}, f32[2,192,256]{2,1,0:T(8,128)}, u32[]{:S(2)}, u32[]{:S(2)}) collective-permute-start(f32[2,192,256]{2,1,0:T(8,128)} %get-tuple-element.1003), channel_id=1, source_target_pairs={{0,1},{1,2},{2,3},{3,4},{4,5},{5,6},{6,7},{7,8},{8,9},{9,10},{10,1... | collective-permute-start | bytes 1179656 | tf_op jit(solution)/shard_map/while/body/eval_jaxpr/ppermute | solution.py:77
  683.5 17.5 %collective-permute-start.5 = (f32[2,192,256]{2,1,0:T(8,128)}, f32[2,192,256]{2,1,0:T(8,128)}, u32[]{:S(2)}, u32[]{:S(2)}) collective-permute-start(f32[2,192,256]{2,1,0:T(8,128)} %get-tuple-element.1004), channel_id=1, source_target_pairs={{0,1},{1,2},{2,3},{3,4},{4,5},{5,6},{6,7},{7,8},{8,9},{9,10},{10,1... | collective-permute-start | bytes 1179656 | tf_op jit(solution)/shard_map/while/body/eval_jaxpr/ppermute | solution.py:77
  686.0 15.0 %collective-permute-start.4 = (f32[2,192,256]{2,1,0:T(8,128)}, f32[2,192,256]{2,1,0:T(8,128)}, u32[]{:S(2)}, u32[]{:S(2)}) collective-permute-start(f32[2,192,256]{2,1,0:T(8,128)} %get-tuple-element.1003), channel_id=1, source_target_pairs={{0,1},{1,2},{2,3},{3,4},{4,5},{5,6},{6,7},{7,8},{8,9},{9,10},{10,1... | collective-permute-start | bytes 1179656 | tf_op jit(solution)/shard_map/while/body/eval_jaxpr/ppermute | solution.py:77
  712.5 17.5 %collective-permute-start.5 = (f32[2,192,256]{2,1,0:T(8,128)}, f32[2,192,256]{2,1,0:T(8,128)}, u32[]{:S(2)}, u32[]{:S(2)}) collective-permute-start(f32[2,192,256]{2,1,0:T(8,128)} %get-tuple-element.1004), channel_id=1, source_target_pairs={{0,1},{1,2},{2,3},{3,4},{4,5},{5,6},{6,7},{7,8},{8,9},{9,10},{10,1... | collective-permute-start | bytes 1179656 | tf_op jit(solution)/shard_map/while/body/eval_jaxpr/ppermute | solution.py:77
  715.0 15.0 %collective-permute-start.4 = (f32[2,192,256]{2,1,0:T(8,128)}, f32[2,192,256]{2,1,0:T(8,128)}, u32[]{:S(2)}, u32[]{:S(2)}) collective-permute-start(f32[2,192,256]{2,1,0:T(8,128)} %get-tuple-element.1003), channel_id=1, source_target_pairs={{0,1},{1,2},{2,3},{3,4},{4,5},{5,6},{6,7},{7,8},{8,9},{9,10},{10,1... | collective-permute-start | bytes 1179656 | tf_op jit(solution)/shard_map/while/body/eval_jaxpr/ppermute | solution.py:77
  742.4 38.3 %collective-permute-start.7 = (bf16[2,192,256]{2,1,0:T(8,128)(2,1)S(1)}, bf16[2,192,256]{2,1,0:T(8,128)(2,1)S(1)}, u32[]{:S(2)}, u32[]{:S(2)}) collective-permute-start(bf16[2,192,256]{2,1,0:T(8,128)(2,1)S(1)} %convert.48), channel_id=1, source_target_pairs={{0,1},{1,2},{2,3},{3,4},{4,5},{5,6},{6,7},{7,8},{8,9},{9,10},{10,1... | collective-permute-start | bytes 589832 | tf_op jit(solution)/shard_map/ppermute | solution.py:77
  745.0 38.1 %collective-permute-start.6 = (f32[2,192,256]{2,1,0:T(8,128)}, f32[2,192,256]{2,1,0:T(8,128)S(1)}, u32[]{:S(2)}, u32[]{:S(2)}) collective-permute-start(f32[2,192,256]{2,1,0:T(8,128)} %get-tuple-element.605), channel_id=1, source_target_pairs={{0,1},{1,2},{2,3},{3,4},{4,5},{5,6},{6,7},{7,8},{8,9},{9,10},{10,1... | collective-permute-start | bytes 1179656 | tf_op jit(solution)/shard_map/ppermute | solution.py:77
  (132 other events, 581.9 us)
Sparse Core Ops, SparseCore 0:
  786.3 415.9 all-reduce.2
where the time goes:
time: 1250 us; the launch traced here: 1230 us
  waiting for transfers between devices  438 us (35%)
  starting transfers between devices  311 us (25%)
  matrix products  241 us (19%)
  local copies, waits for them, and re-layouts  107 us (9%)
  other arithmetic  87.6 us (7%)
  blocking collectives  32.8 us (3%)
  between operations  15.1 us (1%)
    psum x1, waiting for transfers between devices, local_fn(): lax.psum((grad_wq, grad_wk, grad_wv, grad_wo, grad_gain), 'cp')  360 us
    ppermute x92, starting transfers between devices, send_next(): return lax.ppermute(tree_vals, 'cp', next_perm)  311 us
    ppermute x92, waiting for transfers between devices, send_next(): return lax.ppermute(tree_vals, 'cp', next_perm)  77.6 us
    dot_general x16, matrix products, attend_block(): jnp.einsum('cril,cle->crie', exp_scores.astype(jnp.bfloat16), v_blk, pref...  37 us
    dot_general x16, matrix products, attend_grad(): jnp.einsum('cril,crie->cle', attn_p.astype(jnp.bfloat16), da_blk, preferr...  35.8 us
    unnamed x89, local copies, waits for them, and re-layouts  33.1 us
    dot_general x16, matrix products, attend_grad(): jnp.einsum('cril,crie->cle', d_scores, q_blk, preferred_element_type=jnp....  33.1 us
    psum x1, blocking collectives, local_fn(): lax.psum((grad_wq, grad_wk, grad_wv, grad_wo, grad_gain), 'cp')  32.8 us
  transfers between devices with their start and end apart: 93, of which 51 were waited for; matrix products, arithmetic and copies ran while one was open for 6% of the time, Pallas kernels for 0%

commit v1 on v0

v1 whole, which is shorter than its diff:
```python
import functools

import jax
import jax.numpy as jnp
from jax import lax
from jax.experimental import pallas as pl
from jax.experimental.pallas import tpu as pltpu
from jax.sharding import PartitionSpec as P

NORM_EPS = 1e-6
ROPE_BASE = 10000.0
NEG_BIG = -1e30
LOG2_E = 1.4426950408889634
PIECES_PER_BLOCK = 4
VMEM_LIMIT = 60 * 1024 * 1024

NT = (((1,), (1,)), ((), ()))
TN = (((0,), (0,)), ((), ()))
NN = (((1,), (0,)), ((), ()))


def dot(lhs, rhs, dims):
    return lax.dot_general(lhs, rhs, dims, preferred_element_type=jnp.float32)


def rope_tables(positions, head_dim):
    half_dim = head_dim // 2
    inv_freq = ROPE_BASE ** (-(jnp.arange(half_dim, dtype=jnp.float32) * (2.0 / head_dim)))
    angles = positions.astype(jnp.float32)[..., None] * inv_freq
    return jnp.cos(angles), jnp.sin(angles)


def rotate(values, cos_t, sin_t):
    half_dim = values.shape[-1] // 2
    front_half, back_half = values[..., :half_dim], values[..., half_dim:]
    return jnp.concatenate([front_half * cos_t - back_half * sin_t, back_half * cos_t + front_half * sin_t], axis=-1)


def rotate_back(grad_vals, cos_t, sin_t):
    half_dim = grad_vals.shape[-1] // 2
    front_half, back_half = grad_vals[..., :half_dim], grad_vals[..., half_dim:]
    return jnp.concatenate([front_half * cos_t + back_half * sin_t, back_half * cos_t - front_half * sin_t], axis=-1)


def norm_kv_kernel(x_ref, gain_ref, wk_ref, wv_ref, cos_ref, sin_ref, h_ref, kv_ref):
    head_dim = wk_ref.shape[1]
    x_float = x_ref[...].astype(jnp.float32)
    centered = x_float - jnp.mean(x_float, axis=-1, keepdims=True)
    inv_std = lax.rsqrt(jnp.mean(centered * centered, axis=-1, keepdims=True) + NORM_EPS)
    h_norm = (centered * inv_std * gain_ref[...]).astype(jnp.bfloat16)
    h_ref[...] = h_norm
    k_lin = dot(h_norm, wk_ref[...], NN)
    kv_ref[:, :head_dim] = rotate(k_lin, cos_ref[...], sin_ref[...]).astype(jnp.bfloat16)
    kv_ref[:, head_dim:] = dot(h_norm, wv_ref[...], NN).astype(jnp.bfloat16)


def entry_barrier(peers):
    barrier = pltpu.get_barrier_semaphore()
    for peer in peers:
        pl.semaphore_signal(barrier, inc=1, device_id={'cp': peer}, device_id_type=pl.DeviceIdType.MESH)
    pl.semaphore_wait(barrier, len(peers))


def remote(src, dst, send_sem, recv_sem, peer):
    return pltpu.make_async_remote_copy(src_ref=src, dst_ref=dst, send_sem=send_sem, recv_sem=recv_sem,
                                        device_id={'cp': peer}, device_id_type=pl.DeviceIdType.MESH)


def ring_place(n_dev):
    me = lax.axis_index('cp')
    n_chip = n_dev // 2
    chip, core = lax.div(me, 2), lax.rem(me, 2)
    after = lax.rem(chip + 1, n_chip) * 2 + core
    before = lax.rem(chip + n_chip - 1, n_chip) * 2 + core
    partner = chip * 2 + 1 - core
    return n_chip, chip, core, (after, before), partner


def chunk_at(chip, step, way, n_chip):
    if way == 0:
        return lax.rem(chip + 2 * n_chip - 1 - step, n_chip)
    return lax.rem(chip + 1 + step, n_chip)


class RingReduce:
    def __init__(self, n_chip, peers, make_local, local_scr, slots, send_sems, recv_sems):
        self.n_chip, self.peers, self.make_local = n_chip, peers, make_local
        self.local_scr, self.slots, self.send_sems, self.recv_sems = local_scr, slots, send_sems, recv_sems
        self.each = [(sub, way) for sub in range(slots.shape[2]) for way in range(2)]

    def hop(self, step, way, sub, first=False):
        src = self.local_scr.at[way, sub] if first else self.slots.at[way, step - 1, sub]
        return remote(src, self.slots.at[way, step, sub], self.send_sems.at[way, sub], self.recv_sems.at[way, step, sub], self.peers[way])

    def first(self):
        self.make_local(0)
        for sub, way in self.each:
            self.hop(0, way, sub, True).start()

    def middle(self, step, last=False):
        for sub, way in self.each:
            self.hop(step - 1, way, sub, isinstance(step, int) and step == 1).wait_send()
        self.make_local(step)
        for sub, way in self.each:
            self.hop(step - 1, way, sub, isinstance(step, int) and step == 1).wait_recv()
            self.slots[way, step - 1, sub] = self.slots[way, step - 1, sub] + self.local_scr[way, sub]
            if not last:
                self.hop(step, way, sub).start()

    def last(self):
        self.middle(self.n_chip - 1, True)


class RingGather:
    def __init__(self, n_chip, peers, partner, own, place, n_sub, send_sems, recv_sems, mate_send, mate_recv):
        self.n_chip, self.peers, self.partner, self.own, self.place = n_chip, peers, partner, own, place
        self.send_sems, self.recv_sems, self.mate_send, self.mate_recv = send_sems, recv_sems, mate_send, mate_recv
        self.each = [(sub, way) for sub in range(n_sub) for way in range(2)]

    def onward(self, step, way, sub, first=False):
        src = self.own(way, sub) if first else self.place(step, way, sub)
        return remote(src, self.place(step, way, sub), self.send_sems.at[way, sub], self.recv_sems.at[way, step, sub], self.peers[way])

    def across(self, step, way, sub, first=False):
        src = self.own(way, sub) if first else self.place(step, way, sub)
        return remote(src, self.place(step, way, sub), self.mate_send.at[way, sub], self.mate_recv.at[way, step, sub], self.partner)

    def first(self):
        for sub, way in self.each:
            self.onward(0, way, sub, True).start()
            self.across(0, way, sub, True).start()

    def middle(self, step, last=False):
        after_first = isinstance(step, int) and step == 1
        for sub, way in self.each:
            self.onward(step - 1, way, sub, after_first).wait_send()
            self.onward(step - 1, way, sub, after_first).wait_recv()
            if not last:
                self.onward(step, way, sub).start()
            self.across(step - 1, way, sub, after_first).wait_send()
            self.across(step, way, sub).start()

    def last(self):
        self.middle(self.n_chip - 1, True)

    def drain(self):
        for sub, way in self.each:
            self.across(self.n_chip - 1, way, sub).wait_send()

        def body(step, _):
            for sub, way in self.each:
                self.across(step, way, sub).wait_recv()

        lax.fori_loop(0, self.n_chip, body, None)


def owner_at(chip, step, way, n_chip):
    if way == 0:
        return lax.rem(chip + n_chip - step, n_chip)
    return lax.rem(chip + step, n_chip)


def gather_heads_kernel(n_dev, h_ref, dy_ref, kv_ref, wq_ref, wo_ref, cos_ref, sin_ref, all_ref, q_ref, da_ref, wq_buf, wo_buf, w_sems,
                        send_sems, recv_sems, mate_send, mate_recv):
    n_chip, chip, core, peers, partner = ring_place(n_dev)
    n_seq = all_ref.shape[0]
    half_len = all_ref.shape[1] // (2 * n_dev)
    head_dim = wq_buf.shape[2]
    num_heads = q_ref.shape[1]
    q_shape = (q_ref.shape[0], half_len, head_dim)

    def weights(head, slot):
        cols = pl.ds(pl.multiple_of(head * head_dim, head_dim), head_dim)
        return (pltpu.make_async_copy(wq_ref.at[:, cols], wq_buf.at[slot], w_sems.at[0, slot]),
                pltpu.make_async_copy(wo_ref.at[cols, :], wo_buf.at[slot], w_sems.at[1, slot]))

    for copy in weights(0, 0):
        copy.start()
    entry_barrier(peers + (partner,))

    def piece_rows(dev, way):
        piece = dev if way == 0 else 2 * n_dev - 1 - dev
        return pl.ds(pl.multiple_of(piece * half_len, half_len), half_len)

    def place(step, way, seq):
        return all_ref.at[seq, piece_rows(owner_at(chip, step, way, n_chip) * 2 + core, way)]

    def own(way, seq):
        return kv_ref.at[pl.ds((2 * seq + way) * half_len, half_len)]

    ring = RingGather(n_chip, peers, partner, own, place, n_seq, send_sems, recv_sems, mate_send, mate_recv)
    ring.first()
    me = chip * 2 + core
    for seq in range(n_seq):
        for way in range(2):
            all_ref[seq, piece_rows(me, way), :] = kv_ref[(2 * seq + way) * half_len:(2 * seq + way + 1) * half_len, :]

    def project(head, slot):
        @pl.when(head < num_heads)
        def _():
            for copy in weights(head, slot):
                copy.wait()

            @pl.when(head + 1 < num_heads)
            def _():
                for copy in weights(head + 1, 1 - slot):
                    copy.start()

            q_lin = dot(h_ref[...], wq_buf[slot], NN)
            q_ref[:, head] = rotate(q_lin, cos_ref[...], sin_ref[...]).astype(jnp.bfloat16).reshape(q_shape)
            da_ref[:, head] = dot(dy_ref[...], wo_buf[slot], NT).astype(jnp.bfloat16).reshape(q_shape)

    project(0, 0)
    ring.middle(1)

    def body(step, _):
        project(step - 1, lax.rem(step - 1, 2))
        ring.middle(step)

    lax.fori_loop(2, n_chip - 1, body, None)
    project(n_chip - 2, (n_chip - 2) % 2)
    ring.last()
    project(n_chip - 1, (n_chip - 1) % 2)
    ring.drain()


def causal_mask(shape, key_start, query_start, half_len):
    key_idx = key_start + lax.broadcasted_iota(jnp.int32, shape, 0)
    query_idx = query_start + lax.rem(lax.broadcasted_iota(jnp.int32, shape, 1), half_len)
    return key_idx <= query_idx


def attend_kernel(n_dev, q_ref, kv_ref, da_ref, a_ref, lse_ref, delta_ref, acc_scr, max_scr, sum_scr):
    rows, head_dim = q_ref.shape[1:]
    half_len = kv_ref.shape[1] // (2 * n_dev)
    num_heads = rows // half_len
    key_len = PIECES_PER_BLOCK * half_len
    scale = LOG2_E * head_dim ** -0.5
    me = lax.axis_index('cp')
    for group in range(2):
        piece = me if group == 0 else 2 * n_dev - 1 - me
        last = lax.div(piece, PIECES_PER_BLOCK)
        max_scr[...] = jnp.full_like(max_scr, NEG_BIG)
        sum_scr[...] = jnp.zeros_like(sum_scr)
        acc_scr[...] = jnp.zeros_like(acc_scr)

        def block(step, masked, group=group, piece=piece):
            start = pl.multiple_of(step * key_len, key_len)
            keys = pl.ds(start, key_len)
            scores = dot(kv_ref[0, keys, :head_dim], q_ref[group], NT) * scale
            if masked:
                scores = jnp.where(causal_mask(scores.shape, start, piece * half_len, half_len), scores, NEG_BIG)
            old_max = max_scr[...]
            new_max = jnp.maximum(old_max, jnp.max(scores, axis=0, keepdims=True))
            rescale = jnp.exp2(old_max - new_max)
            probs = jnp.exp2(scores - new_max)
            max_scr[...] = new_max
            sum_scr[...] = sum_scr[...] * rescale + jnp.sum(probs, axis=0, keepdims=True)
            acc_scr[...] = acc_scr[...] * rescale + dot(kv_ref[0, keys, head_dim:], probs.astype(jnp.bfloat16), TN)

        lax.fori_loop(0, last, lambda step, _: block(step, False), None)
        block(last, True)
        attn = (acc_scr[...] / sum_scr[...]).T.astype(jnp.bfloat16)
        lse_ref[group] = max_scr[...] + jnp.log2(sum_scr[...])
        prod = attn.astype(jnp.float32) * da_ref[group].astype(jnp.float32)
        prod = prod[:, :head_dim // 2] + prod[:, head_dim // 2:]
        delta_ref[group] = jnp.sum(prod.T, axis=0, keepdims=True)
        for head in range(num_heads):
            a_ref[group, :, head * head_dim:(head + 1) * head_dim] = attn[head * half_len:(head + 1) * half_len, :]


def attend_grad_kernel(n_dev, q_ref, kv_ref, da_ref, lse_ref, delta_ref, cos_ref, sin_ref, a_ref, dy_ref, z_ref, wo_ref,
                       q_scr, da_scr, kv_scr, dq_scr, dkv_scr, mate_scr, kv_local, kv_slots, a_scr, dy_scr, wo_local, wo_slots,
                       load_sems, swap_send, swap_recv, kv_send, kv_recv, mate_send, mate_recv, wo_send, wo_recv):
    n_chip, chip, core, peers, partner = ring_place(n_dev)
    me = chip * 2 + core
    rows, head_dim = q_scr.shape[1:]
    n_seq, seq_len, kv_width = dkv_scr.shape
    half_len = seq_len // (2 * n_dev)
    num_heads = rows // half_len
    q_width = num_heads * head_dim
    n_rows = a_ref.shape[0]
    key_len = PIECES_PER_BLOCK * half_len
    scale = LOG2_E * head_dim ** -0.5
    dy_cols = dy_scr.shape[1]
    mine, other = pl.ds(0, n_rows), pl.ds(n_rows, n_rows)

    def cols(which, size):
        return pl.ds(pl.multiple_of(which * size, size), size)

    loads = [
        pltpu.make_async_copy(a_ref, a_scr.at[mine], load_sems.at[0]),
        pltpu.make_async_copy(dy_ref.at[:, cols(core, dy_cols)], dy_scr.at[mine], load_sems.at[1]),
        pltpu.make_async_copy(q_ref, q_scr, load_sems.at[2]),
        pltpu.make_async_copy(da_ref, da_scr, load_sems.at[3]),
        pltpu.make_async_copy(kv_ref, kv_scr, load_sems.at[4]),
    ]
    for load in loads:
        load.start()
    entry_barrier(peers + (partner,))
    swaps = [
        remote(a_ref, a_scr.at[other], swap_send.at[0], swap_recv.at[0], partner),
        remote(dy_ref.at[:, cols(1 - core, dy_cols)], dy_scr.at[other], swap_send.at[1], swap_recv.at[1], partner),
    ]
    for swap in swaps:
        swap.start()
    dkv_scr[...] = jnp.zeros_like(dkv_scr)
    loads[0].wait()
    loads[1].wait()
    for swap in swaps:
        swap.wait_recv()

    def wo_local_term(step):
        n_sub, sub_len = wo_local.shape[1:3]
        way_len = n_sub * sub_len
        for way in range(2):
            first = chunk_at(chip, step, way, n_chip) * (2 * way_len) + way * way_len
            part = dot(a_scr[:, pl.ds(pl.multiple_of(first, way_len), way_len)], dy_scr[...], TN)
            for sub in range(n_sub):
                wo_local[way, sub] = part[sub * sub_len:(sub + 1) * sub_len, :]

    def piece_rows(dev, sub):
        piece = dev if sub == 0 else 2 * n_dev - 1 - dev
        return pl.ds(pl.multiple_of(piece * half_len, half_len), half_len)

    def mate_copy(step, way, sub):
        dev = chunk_at(chip, step, way, n_chip) * 2 + 1 - core
        return remote(dkv_scr.at[way, piece_rows(dev, sub)], mate_scr.at[way, step, sub], mate_send.at[way, step, sub], mate_recv.at[way, step, sub], partner)

    def kv_local_term(step):
        for sub in range(2):
            for way in range(2):
                mate_copy(step, way, sub).wait_recv()
                dev = chunk_at(chip, step, way, n_chip) * 2 + core
                kv_local[way, sub] = dkv_scr[way, piece_rows(dev, sub), :] + mate_scr[way, step, sub]

    wo_ring = RingReduce(n_chip, peers, wo_local_term, wo_local, wo_slots, wo_send, wo_recv)
    kv_ring = RingReduce(n_chip, peers, kv_local_term, kv_local, kv_slots, kv_send, kv_recv)

    def attend_seq(seq):
        def one_group(group, _):
            index = 2 * seq + group
            piece = me + group * (2 * n_dev - 1 - 2 * me)
            last = lax.div(piece, PIECES_PER_BLOCK)
            dq_scr[...] = jnp.zeros_like(dq_scr)

            def block(step, masked):
                start = pl.multiple_of(step * key_len, key_len)
                keys = pl.ds(start, key_len)
                k_blk, v_blk = kv_scr[seq, keys, :head_dim], kv_scr[seq, keys, head_dim:]
                probs = jnp.exp2(dot(k_blk, q_scr[index], NT) * scale - lse_ref[index])
                if masked:
                    probs = jnp.where(causal_mask(probs.shape, start, piece * half_len, half_len), probs, 0.0)
                d_scores = (probs * (dot(v_blk, da_scr[index], NT) - delta_ref[index])).astype(jnp.bfloat16)
                dq_scr[...] += dot(k_blk, d_scores, TN)
                dkv_scr[seq, keys, :head_dim] += dot(d_scores, q_scr[index], NN) * head_dim ** -0.5
                dkv_scr[seq, keys, head_dim:] += dot(probs.astype(jnp.bfloat16), da_scr[index], NN)

            lax.fori_loop(0, last, lambda step, _: block(step, False), None)
            block(last, True)
            dq = dq_scr[...].T * head_dim ** -0.5
            out_rows = pl.ds(pl.multiple_of(index * half_len, half_len), half_len)
            cos_t, sin_t = cos_ref[out_rows, :], sin_ref[out_rows, :]
            for head in range(num_heads):
                dq_head = dq[head * half_len:(head + 1) * half_len, :]
                z_ref[out_rows, head * head_dim:(head + 1) * head_dim] = rotate_back(dq_head, cos_t, sin_t).astype(jnp.bfloat16)

        lax.fori_loop(0, 2, one_group, None)

        def send_mate(step, _):
            for sub in range(2):
                mate_copy(step, seq, sub).start()

        lax.fori_loop(0, n_chip, send_mate, None)

    wo_ring.first()
    for load in loads[2:]:
        load.wait()
    attend_seq(0)
    wo_ring.middle(1)
    attend_seq(1)
    wo_ring.middle(2)
    kv_ring.first()
    wo_ring.middle(3)
    kv_ring.middle(1)

    def both(step, _):
        wo_ring.middle(step + 2)
        kv_ring.middle(step)

    lax.fori_loop(2, n_chip - 3, both, None)
    wo_ring.last()
    for way in range(2):
        for sub in range(wo_local.shape[1]):
            wo_ref[way, sub] = wo_slots[way, n_chip - 2, sub]
    kv_ring.middle(n_chip - 3)
    kv_ring.middle(n_chip - 2)
    kv_ring.last()
    for way in range(2):
        for sub in range(2):
            out_rows = slice((2 * way + sub) * half_len, (2 * way + sub + 1) * half_len)
            total = kv_slots[way, n_chip - 2, sub]
            z_ref[out_rows, q_width:q_width + head_dim] = rotate_back(total[:, :head_dim], cos_ref[out_rows, :], sin_ref[out_rows, :]).astype(jnp.bfloat16)
            z_ref[out_rows, q_width + head_dim:] = total[:, head_dim:].astype(jnp.bfloat16)

    def mates_sent(step, _):
        for way in range(2):
            for sub in range(2):
                mate_copy(step, way, sub).wait_send()

    lax.fori_loop(0, n_chip, mates_sent, None)
    for swap in swaps:
        swap.wait_send()


def finish_kernel(n_dev, h_ref, z_ref, wo_part_ref, a_ref, x_ref, dy_ref, gain_ref, wq_ref, wo_ref, wk_ref, wv_ref,
                  gz_ref, gwo_ref, y_ref, dx_ref, ggain_ref,
                  h_scr, z_scr, zf_scr, a_scr, x_scr, dy_scr, dh_scr, wq_buf, wo_buf, gain_slots, local_scr, slots,
                  load_sems, w_sems, swap_send, swap_recv, send_sems, recv_sems, g1_send, g1_recv, m1_send, m1_recv,
                  g2_send, g2_recv, m2_send, m2_recv, keep_sems, gain_send, gain_recv):
    n_chip, chip, core, peers, partner = ring_place(n_dev)
    me = chip * 2 + core
    n_rows, model_dim = h_ref.shape
    core_width = z_scr.shape[1]
    q_width = a_ref.shape[1]
    head_dim = wk_ref.shape[1]
    n_sub, sub_len = local_scr.shape[1:3]
    way_len = n_sub * sub_len
    wo_sub_len, wo_width = wo_part_ref.shape[2:]
    wo_way_len = n_sub * wo_sub_len
    blk = model_dim // n_chip
    mine, other = pl.ds(0, n_rows), pl.ds(n_rows, n_rows)

    def cols(which, size):
        return pl.ds(pl.multiple_of(which * size, size), size)

    def wq_load(index, slot):
        return pltpu.make_async_copy(wq_ref.at[cols(index, blk), :], wq_buf.at[slot], w_sems.at[0, slot])

    def wo_load(index, slot):
        return pltpu.make_async_copy(wo_ref.at[:, cols(index, blk)], wo_buf.at[slot], w_sems.at[1, slot])

    loads = [
        pltpu.make_async_copy(h_ref, h_scr.at[mine], load_sems.at[0]),
        pltpu.make_async_copy(z_ref.at[:, cols(core, core_width)], z_scr.at[mine], load_sems.at[1]),
        pltpu.make_async_copy(z_ref, zf_scr, load_sems.at[2]),
        pltpu.make_async_copy(a_ref, a_scr, load_sems.at[3]),
        pltpu.make_async_copy(x_ref, x_scr, load_sems.at[4]),
        pltpu.make_async_copy(dy_ref, dy_scr, load_sems.at[5]),
    ]
    for load in loads:
        load.start()
    wq_load(0, 0).start()
    wo_load(0, 0).start()
    barrier = pltpu.get_barrier_semaphore()
    for offset in range(1, n_dev):
        pl.semaphore_signal(barrier, inc=1, device_id={'cp': lax.rem(me + offset, n_dev)}, device_id_type=pl.DeviceIdType.MESH)
    pl.semaphore_wait(barrier, n_dev - 1)

    def wo_place(step, way, sub):
        first = owner_at(chip, step, way, n_chip) * (2 * wo_way_len) + way * wo_way_len + sub * wo_sub_len
        return gwo_ref.at[pl.ds(pl.multiple_of(first, wo_sub_len), wo_sub_len), cols(core, wo_width)]

    def z_place(step, way, sub):
        first = owner_at(chip, step, way, n_chip) * (2 * way_len) + way * way_len + sub * sub_len
        return gz_ref.at[pl.ds(pl.multiple_of(first, sub_len), sub_len), cols(core, core_width)]

    swaps = [
        remote(h_ref, h_scr.at[other], swap_send.at[0], swap_recv.at[0], partner),
        remote(z_ref.at[:, cols(1 - core, core_width)], z_scr.at[other], swap_send.at[1], swap_recv.at[1], partner),
    ]
    for swap in swaps:
        swap.start()
    wo_gather = RingGather(n_chip, peers, partner, lambda way, sub: wo_part_ref.at[way, sub], wo_place, n_sub, g1_send, g1_recv, m1_send, m1_recv)
    z_gather = RingGather(n_chip, peers, partner, lambda way, sub: slots.at[way, n_chip - 2, sub], z_place, n_sub, g2_send, g2_recv, m2_send, m2_recv)
    keeps = ([pltpu.make_async_copy(wo_part_ref.at[way, sub], wo_place(0, way, sub), keep_sems.at[0, way, sub]) for sub, way in wo_gather.each],
             [pltpu.make_async_copy(slots.at[way, n_chip - 2, sub], z_place(0, way, sub), keep_sems.at[1, way, sub]) for sub, way in wo_gather.each])
    wo_gather.first()
    for keep in keeps[0]:
        keep.start()

    def local_term(step):
        for way in range(2):
            first = chunk_at(chip, step, way, n_chip) * (2 * way_len) + way * way_len
            part = dot(h_scr[:, pl.ds(pl.multiple_of(first, way_len), way_len)], z_scr[...], TN)
            for sub in range(n_sub):
                local_scr[way, sub] = part[sub * sub_len:(sub + 1) * sub_len, :]

    z_ring = RingReduce(n_chip, peers, local_term, local_scr, slots, send_sems, recv_sems)

    def d_hidden(index, slot):
        wq_load(index, slot).wait()

        @pl.when(index + 1 < n_chip)
        def _():
            wq_load(index + 1, 1 - slot).start()

        rows = cols(index, blk)
        dh_scr[:, rows] = (dot(zf_scr[:, :q_width], wq_buf[slot], NT) + dot(zf_scr[:, q_width:q_width + head_dim], wk_ref[rows, :], NT)
                           + dot(zf_scr[:, q_width + head_dim:], wv_ref[rows, :], NT))

    def out_block(index, slot):
        wo_load(index, slot).wait()

        @pl.when(index + 1 < n_chip)
        def _():
            wo_load(index + 1, 1 - slot).start()

        where = cols(index, blk)
        o_blk = dot(a_scr[...], wo_buf[slot], NN).astype(jnp.bfloat16)
        y_ref[:, where] = (x_scr[:, where].astype(jnp.float32) + o_blk.astype(jnp.float32)).astype(jnp.bfloat16)

    def norm_grad(index, _):
        rows = pl.ds(pl.multiple_of(index * 32, 32), 32)
        x_float = x_scr[rows, :].astype(jnp.float32)
        centered = x_float - jnp.mean(x_float, axis=-1, keepdims=True)
        inv_std = lax.rsqrt(jnp.mean(centered * centered, axis=-1, keepdims=True) + NORM_EPS)
        x_hat = centered * inv_std
        d_h = dh_scr[rows, :]
        gain_slots[me] += jnp.sum(d_h * x_hat, axis=0, keepdims=True)
        d_hat = d_h * gain_ref[...]
        mean_d = jnp.mean(d_hat, axis=-1, keepdims=True)
        mean_dx = jnp.mean(d_hat * x_hat, axis=-1, keepdims=True)
        dx_ref[rows, :] = (dy_scr[rows, :].astype(jnp.float32) + inv_std * (d_hat - mean_d - x_hat * mean_dx)).astype(jnp.bfloat16)

    def gain_copy(offset):
        return remote(gain_slots.at[me], gain_slots.at[me], gain_send.at[offset], gain_recv.at[offset], lax.rem(me + offset, n_dev))

    loads[0].wait()
    loads[1].wait()
    for swap in swaps:
        swap.wait_recv()
    z_ring.first()
    for load in loads[2:]:
        load.wait()
    wo_gather.middle(1)
    z_ring.middle(1)
    d_hidden(0, 0)

    def phase_one(step, _):
        wo_gather.middle(step)
        z_ring.middle(step)
        d_hidden(step - 1, lax.rem(step - 1, 2))

    lax.fori_loop(2, n_chip - 1, phase_one, None)
    wo_gather.last()
    z_ring.last()
    z_gather.first()
    for keep in keeps[1]:
        keep.start()
    d_hidden(n_chip - 2, (n_chip - 2) % 2)
    d_hidden(n_chip - 1, (n_chip - 1) % 2)
    gain_slots[me] = jnp.zeros(gain_slots.shape[1:], jnp.float32)
    lax.fori_loop(0, n_rows // 32, norm_grad, None)
    for offset in range(1, n_dev):
        gain_copy(offset).start()
    z_gather.middle(1)
    out_block(0, 0)
    out_block(1, 1)

    def phase_two(step, _):
        z_gather.middle(step)
        out_block(step, lax.rem(step, 2))

    lax.fori_loop(2, n_chip - 1, phase_two, None)
    out_block(n_chip - 1, (n_chip - 1) % 2)
    z_gather.last()
    for offset in range(1, n_dev):
        gain_copy(offset).wait_recv()
    total = gain_slots[0]
    for dev in range(1, n_dev):
        total = total + gain_slots[dev]
    ggain_ref[...] = total
    wo_gather.drain()
    z_gather.drain()
    for keep in keeps[0] + keeps[1]:
        keep.wait()
    for swap in swaps:
        swap.wait_send()
    for offset in range(1, n_dev):
        gain_copy(offset).wait_send()


def solution(mesh):
    n_dev = mesh.shape['cp']
    n_chip, n_sub = n_dev // 2, 2

    def local_fn(tokens, positions, norm_gain, w_query, w_key, w_value, w_out, d_out):
        n_seq, blk_len, model_dim = tokens.shape
        head_dim = w_key.shape[1]
        num_heads = w_query.shape[1] // head_dim
        q_width, kv_width = num_heads * head_dim, 2 * head_dim
        half_len, half = blk_len // 2, head_dim // 2
        n_rows, n_groups = n_seq * blk_len, 2 * n_seq
        rows = num_heads * half_len
        seq_len = n_dev * blk_len
        bf16, f32 = jnp.bfloat16, jnp.float32
        dma = pltpu.SemaphoreType.DMA
        vmem = pl.BlockSpec(memory_space=pltpu.VMEM)
        hbm = pl.BlockSpec(memory_space=pl.ANY)
        params = pltpu.CompilerParams(vmem_limit_bytes=VMEM_LIMIT)

        def comm(ident):
            return pltpu.CompilerParams(vmem_limit_bytes=VMEM_LIMIT, collective_id=ident, has_side_effects=True)

        def shape(*dims, dtype=bf16):
            return jax.ShapeDtypeStruct(dims, dtype)

        def gather_sems():
            return [dma((2, n_sub)), dma((2, n_chip - 1, n_sub)), dma((2, n_sub)), dma((2, n_chip, n_sub))]

        x_flat = tokens.reshape(n_rows, model_dim)
        dy_flat = d_out.reshape(n_rows, model_dim)
        gain_row = norm_gain.reshape(1, model_dim)
        cos_t, sin_t = rope_tables(positions.reshape(n_rows), head_dim)
        h_flat, kv_flat = pl.pallas_call(
            norm_kv_kernel,
            out_shape=(shape(n_rows, model_dim), shape(n_rows, kv_width)),
            compiler_params=params, name='norm_kv',
        )(x_flat, gain_row, w_key, w_value, cos_t, sin_t)

        kv_all, q_heads, da_heads = pl.pallas_call(
            functools.partial(gather_heads_kernel, n_dev),
            in_specs=[vmem, vmem, vmem, hbm, hbm, vmem, vmem],
            out_specs=[vmem, vmem, vmem],
            out_shape=(shape(n_seq, seq_len, kv_width), shape(n_groups, num_heads, half_len, head_dim), shape(n_groups, num_heads, half_len, head_dim)),
            scratch_shapes=[pltpu.VMEM((2, model_dim, head_dim), bf16), pltpu.VMEM((2, head_dim, model_dim), bf16), dma((2, 2))] + gather_sems(),
            compiler_params=comm(0), name='gather_heads',
        )(h_flat, dy_flat, kv_flat, w_query, w_out, cos_t, sin_t)
        q_rows = q_heads.reshape(n_groups, rows, head_dim)
        da_rows = da_heads.reshape(n_groups, rows, head_dim)

        q_spec = pl.BlockSpec((2, rows, head_dim), lambda s: (s, 0, 0))
        kv_spec = pl.BlockSpec((1, seq_len, kv_width), lambda s: (s, 0, 0))
        tok_spec = pl.BlockSpec((2, half_len, q_width), lambda s: (s, 0, 0))
        stat_spec = pl.BlockSpec((2, 1, rows), lambda s: (s, 0, 0))
        attn, lse, delta = pl.pallas_call(
            functools.partial(attend_kernel, n_dev),
            grid=(n_seq,),
            in_specs=[q_spec, kv_spec, q_spec],
            out_specs=[tok_spec, stat_spec, stat_spec],
            out_shape=(shape(n_groups, half_len, q_width), shape(n_groups, 1, rows, dtype=f32), shape(n_groups, 1, rows, dtype=f32)),
            scratch_shapes=[pltpu.VMEM((head_dim, rows), f32), pltpu.VMEM((1, rows), f32), pltpu.VMEM((1, rows), f32)],
            compiler_params=params, name='attend',
        )(q_rows, kv_all, da_rows)
        attn_flat = attn.reshape(n_rows, q_width)

        z_width = q_width + kv_width
        wo_cols, wo_sub = model_dim // 2, q_width // (2 * n_chip * n_sub)
        z_flat, wo_part = pl.pallas_call(
            functools.partial(attend_grad_kernel, n_dev),
            in_specs=[hbm, hbm, hbm, vmem, vmem, vmem, vmem, hbm, hbm],
            out_specs=[vmem, vmem],
            out_shape=(shape(n_rows, z_width), shape(2, n_sub, wo_sub, wo_cols, dtype=f32)),
            scratch_shapes=[pltpu.VMEM((n_groups, rows, head_dim), bf16), pltpu.VMEM((n_groups, rows, head_dim), bf16),
                            pltpu.VMEM((n_seq, seq_len, kv_width), bf16), pltpu.VMEM((head_dim, rows), f32),
                            pltpu.VMEM((n_seq, seq_len, kv_width), f32), pltpu.VMEM((2, n_chip, 2, half_len, kv_width), f32),
                            pltpu.VMEM((2, 2, half_len, kv_width), f32), pltpu.VMEM((2, n_chip - 1, 2, half_len, kv_width), f32),
                            pltpu.VMEM((2 * n_rows, q_width), bf16), pltpu.VMEM((2 * n_rows, wo_cols), bf16),
                            pltpu.VMEM((2, n_sub, wo_sub, wo_cols), f32), pltpu.VMEM((2, n_chip - 1, n_sub, wo_sub, wo_cols), f32),
                            dma((5,)), dma((2,)), dma((2,)), dma((2, 2)), dma((2, n_chip - 1, 2)), dma((2, n_chip, 2)), dma((2, n_chip, 2)),
                            dma((2, n_sub)), dma((2, n_chip - 1, n_sub))],
            compiler_params=comm(1), name='attend_grad',
        )(q_rows, kv_all, da_rows, lse, delta, cos_t, sin_t, attn_flat, dy_flat)

        core_width, sub_len = z_width // 2, model_dim // (2 * n_chip * n_sub)
        blk = model_dim // n_chip
        grad_z, grad_wo, out_y, grad_x, grad_gain = pl.pallas_call(
            functools.partial(finish_kernel, n_dev),
            in_specs=[hbm] * 6 + [vmem, hbm, hbm, vmem, vmem],
            out_specs=[hbm, hbm, vmem, vmem, vmem],
            out_shape=(shape(model_dim, z_width, dtype=f32), shape(q_width, model_dim, dtype=f32), shape(n_rows, model_dim), shape(n_rows, model_dim),
                       shape(1, model_dim, dtype=f32)),
            scratch_shapes=[pltpu.VMEM((2 * n_rows, model_dim), bf16), pltpu.VMEM((2 * n_rows, core_width), bf16), pltpu.VMEM((n_rows, z_width), bf16),
                            pltpu.VMEM((n_rows, q_width), bf16), pltpu.VMEM((n_rows, model_dim), bf16), pltpu.VMEM((n_rows, model_dim), bf16),
                            pltpu.VMEM((n_rows, model_dim), f32), pltpu.VMEM((2, blk, q_width), bf16), pltpu.VMEM((2, q_width, blk), bf16),
                            pltpu.VMEM((n_dev, 1, model_dim), f32), pltpu.VMEM((2, n_sub, sub_len, core_width), f32),
                            pltpu.VMEM((2, n_chip - 1, n_sub, sub_len, core_width), f32),
                            dma((6,)), dma((2, 2)), dma((2,)), dma((2,)), dma((2, n_sub)), dma((2, n_chip - 1, n_sub))]
            + gather_sems() + gather_sems() + [dma((2, 2, n_sub)), dma((n_dev,)), dma((n_dev,))],
            compiler_params=comm(2), name='finish',
        )(h_flat, z_flat, wo_part, attn_flat, x_flat, dy_flat, gain_row, w_query, w_out, w_key, w_value)
        grad_wq, grad_wk, grad_wv = grad_z[:, :q_width], grad_z[:, q_width:q_width + head_dim], grad_z[:, q_width + head_dim:]
        return out_y.reshape(tokens.shape), grad_x.reshape(tokens.shape), grad_wq, grad_wk, grad_wv, grad_wo, grad_gain.reshape(model_dim)

    seq_spec = P('dp', 'cp', None)
    rep_spec = P(None, None)
    part_spec = P('dp', None)
    return jax.shard_map(local_fn, mesh=mesh,
                         in_specs=(seq_spec, P('dp', 'cp'), P(None), rep_spec, rep_spec, rep_spec, rep_spec, seq_spec),
                         out_specs=(seq_spec, seq_spec, part_spec, part_spec, part_spec, part_spec, P('dp')),
                         check_vma=False)
```

time: 1250 us -> 555 us (0.44); the launches traced: 1230 us -> 555 us
  Pallas kernels: 0 us -> 523 us
  waiting for transfers between devices: 438 us -> 0 us
  starting transfers between devices: 311 us -> 0 us
  matrix products: 241 us -> 0 us
  other arithmetic: 87.6 us -> 2.2 us
  local copies, waits for them, and re-layouts: 107 us -> 29.1 us
  blocking collectives: 32.8 us -> 0 us
  between operations: 15.1 us -> 0.7 us
    pallas_call x0 -> x5, Pallas kernels: none -> 523 us  [the longest x1 295 us: local_fn(): pl.pallas_call(functools.partial(finish_kernel, n_dev), in_specs=[hbm] *...]
    psum x1 -> x0, waiting for transfers between devices: 360 us -> none  [local_fn(): lax.psum((grad_wq, grad_wk, grad_wv, grad_wo, grad_gain), 'cp')]
    ppermute x92 -> x0, starting transfers between devices: 311 us -> none  [send_next(): return lax.ppermute(tree_vals, 'cp', next_perm)]
    dot_general x123 -> x0, matrix products: 241 us -> none  [the longest x16 37 us: attend_block(): jnp.einsum('cril,cle->crie', exp_scores.astype(jnp.bfloat16), v_blk, pref...]
    ppermute x92 -> x0, waiting for transfers between devices: 77.6 us -> none  [send_next(): return lax.ppermute(tree_vals, 'cp', next_perm)]
    concatenate x46 -> x0, other arithmetic: 55.9 us -> none  [the longest x14 26.2 us: grad_after(): jnp.concatenate([dq_in[:, :half_len], dq_in[:, half_len:] + dq_part], axi...]
    psum x1 -> x0, blocking collectives: 32.8 us -> none  [local_fn(): lax.psum((grad_wq, grad_wk, grad_wv, grad_wo, grad_gain), 'cp')]
    another operation x32 -> x0, local copies, waits for them, and re-layouts: 26.8 us -> none
  transfers between devices with their start and end apart: 93 -> 0, of which waited for: 51 -> 0; matrix products, arithmetic and copies ran while one was open for 6% -> 0% of each run, Pallas kernels for 0% -> 0%
where the time goes in v1:
time: 555 us
  Pallas kernels  523 us (94%)
  local copies, waits for them, and re-layouts  29.1 us (5%)
    pallas_call x1, Pallas kernels, local_fn(): pl.pallas_call(functools.partial(finish_kernel, n_dev), in_specs=[hbm] *...  295 us
    pallas_call x1, Pallas kernels, local_fn(): pl.pallas_call(functools.partial(attend_grad_kernel, n_dev), in_specs=[hb...  153 us
    pallas_call x1, Pallas kernels, local_fn(): pl.pallas_call(functools.partial(gather_heads_kernel, n_dev), in_specs=[v...  48.7 us
    pallas_call x1, Pallas kernels, local_fn(): pl.pallas_call(functools.partial(attend_kernel, n_dev), grid=(n_seq,), in...  22.7 us
    slice x1, local copies, waits for them, and re-layouts, local_fn(): grad_z[:, :q_width]  13.5 us

profile of v1, /device:TPU:21, one launch (start us, length us, event | category | flops | bytes accessed | tf_op | source)
XLA Modules:
  0.0 555.0 jit_solution(1615204762753126178)
XLA Ops:
  0.6 0.7 convert_element_type.10
  1.3 0.1 convert_element_type.11
  1.4 1.5 multiply_sine_fusion
  2.9 4.6 norm_kv.1
  7.6 48.7 %gather_heads.1 = (bf16[2,3072,512]{2,1,0:T(8,128)(2,1)}, bf16[4,8,96,256]{3,2,1,0:T(8,128)(2,1)}, bf16[4,8,96,256]{3,2,1,0:T(8,128)(2,1)}) custom-call(bf16[384,2048]{1,0:T(8,128)(2,1)} %get-tuple-element.22.h_ref, bf16[384,2048]{1,0:T(8,128)(2,1)} %bitcast.11, bf16[384,512]{1,0:T(8,128)(2,1)} %get-tuple-element.23.kv_ref, bf16[2048,2048]{1,0:T(8,128)(2,1)} %wq_ref.3, ...), custom_call_target="tpu_custom_call" | custom-call | tf_op jit(solution)/shard_map/gather_heads/pallas_call | solution.py:622
  56.2 22.7 %attend.1 = (bf16[4,96,2048]{2,1,0:T(8,128)(2,1)}, f32[4,1,768]{2,1,0:T(1,128)}, f32[4,1,768]{2,1,0:T(1,128)}) custom-call(bf16[4,768,256]{2,1,0:T(8,128)(2,1)} %bitcast.14, bf16[2,3072,512]{2,1,0:T(8,128)(2,1)} %get-tuple-element.25.kv_ref, bf16[4,768,256]{2,1,0:T(8,128)(2,1)} %bitcast.16), custom_call_target="tpu_custom_call" | custom-call | tf_op jit(solution)/shard_map/attend/pallas_call | solution.py:637
  78.9 152.5 %attend_grad.1 = (bf16[384,2560]{1,0:T(8,128)(2,1)}, f32[2,2,64,1024]{3,2,1,0:T(8,128)}) custom-call(bf16[4,768,256]{2,1,0:T(8,128)(2,1)} %bitcast.15, bf16[2,3072,512]{2,1,0:T(8,128)(2,1)} %get-tuple-element.25.kv_ref, bf16[4,768,256]{2,1,0:T(8,128)(2,1)} %bitcast.17, f32[4,1,768]{2,1,0:T(1,128)} %get-tuple-element.27.lse_ref, ...), custom_call_target="tpu_custom_call" | custom-call | tf_op jit(solution)/shard_map/attend_grad/pallas_call | solution.py:650
  231.4 294.5 %finish.1 = (f32[2048,2560]{1,0:T(8,128)}, f32[2048,2048]{1,0:T(8,128)}, bf16[384,2048]{1,0:T(8,128)(2,1)}, bf16[384,2048]{1,0:T(8,128)(2,1)}, f32[1,2048]{1,0:T(1,128)}) custom-call(bf16[384,2048]{1,0:T(8,128)(2,1)} %get-tuple-element.22.h_ref, bf16[384,2560]{1,0:T(8,128)(2,1)} %get-tuple-element.30.z_ref, ...), custom_call_target="tpu_custom_call" | custom-call | tf_op jit(solution)/shard_map/finish/pallas_call | solution.py:668
  525.9 0.0 slice-start
  525.9 4.7 fusion
  530.6 0.0 copy-start.1
  530.6 0.0 slice-start.1
  530.6 0.0 slice-start.2
  530.6 0.0 slice-start.3
  530.6 13.5 %slice.9 = f32[2048,2048]{1,0:T(8,128)} slice(f32[2048,2560]{1,0:T(8,128)} %get-tuple-element.34), slice={[0:2048], [0:2048]} | slice | bytes 33554432 | tf_op jit(solution)/shard_map/slice | solution.py:683
  544.1 0.0 copy-start
  544.1 0.0 copy-done.1
  544.2 1.1 copy.19
  545.3 1.7 copy-done
  547.0 1.1 copy.20
  548.2 0.0 slice-done
  548.2 0.0 slice-done.1
  548.2 0.0 slice-done.2
  548.2 0.0 slice-done.3
  548.2 0.0 copy-start.2
  548.2 6.2 %copy.21 = f32[2048,2048]{1,0:T(8,128)} copy(f32[2048,2048]{1,0:T(8,128)S(1)} %bitcast.10) | data formatting | bytes 33554432
  554.4 0.0 copy-done.2
  554.4 0.6 copy.22
  (2 shorter events, 0.0 us)
Async XLA Ops:
  525.9 22.2 %slice-start = ((s8[16777216]{0:T(1024)(128)(4,1)}), s8[4194304]{0:T(1024)(128)(4,1)S(1)}, s32[]{:S(2)}) async-start(s8[16777216]{0:T(1024)(128)(4,1)} %bitcast.9), calls=%async_computation | async-start | bytes 8388608
  530.6 13.5 %copy-start.1 = (bf16[384,2048]{1,0:T(8,128)(2,1)S(1)}, bf16[384,2048]{1,0:T(8,128)(2,1)}, u32[]{:S(2)}) copy-start(bf16[384,2048]{1,0:T(8,128)(2,1)} %get-tuple-element.32) | copy-start | bytes 4718596
  530.6 17.5 %slice-start.1 = ((s8[16777216]{0:T(1024)(128)(4,1)}), s8[4194304]{0:T(1024)(128)(4,1)S(1)}, s32[]{:S(2)}) async-start(s8[16777216]{0:T(1024)(128)(4,1)} %bitcast.9), calls=%async_computation.1 | async-start | bytes 8388608
  530.6 17.5 %slice-start.2 = ((s8[16777216]{0:T(1024)(128)(4,1)}), s8[4194304]{0:T(1024)(128)(4,1)S(1)}, s32[]{:S(2)}) async-start(s8[16777216]{0:T(1024)(128)(4,1)} %bitcast.9), calls=%async_computation.2 | async-start | bytes 8388608
  530.6 17.5 %slice-start.3 = ((s8[16777216]{0:T(1024)(128)(4,1)}), s8[4194304]{0:T(1024)(128)(4,1)S(1)}, s32[]{:S(2)}) async-start(s8[16777216]{0:T(1024)(128)(4,1)} %bitcast.9), calls=%async_computation.3 | async-start | bytes 8388608
  544.1 2.9 copy-start
  548.2 6.2 %copy-start.2 = (f32[1,2048]{1,0:T(1,128)S(1)}, f32[1,2048]{1,0:T(1,128)}, u32[]{:S(2)}) copy-start(f32[1,2048]{1,0:T(1,128)} %get-tuple-element.36) | copy-start | bytes 24580

commit v2 on v1

--- a/solution.py
+++ b/solution.py
@@ -160,20 +160,32 @@
     return lax.rem(chip + step, n_chip)
 
 
-def gather_heads_kernel(n_dev, h_ref, dy_ref, kv_ref, wq_ref, wo_ref, cos_ref, sin_ref, all_ref, q_ref, da_ref, wq_buf, wo_buf, w_sems,
-                        send_sems, recv_sems, mate_send, mate_recv):
+def causal_mask(shape, key_start, query_start, half_len):
+    key_idx = key_start + lax.broadcasted_iota(jnp.int32, shape, 0)
+    query_idx = query_start + lax.rem(lax.broadcasted_iota(jnp.int32, shape, 1), half_len)
+    return key_idx <= query_idx
+
+
+def forward_kernel(n_dev, kv_ref, cos_ref, sin_ref, h_ref, dy_ref, wq_ref, wo_ref, all_ref, q_ref, da_ref, a_ref, lse_ref, delta_ref,
+                   h_scr, dy_scr, kv_scr, q_scr, da_scr, qt_scr, a_scr, acc_scr, max_scr, sum_scr, wq_buf, wo_buf,
+                   load_sems, out_sems, w_sems, send_sems, recv_sems, mate_send, mate_recv):
     n_chip, chip, core, peers, partner = ring_place(n_dev)
-    n_seq = all_ref.shape[0]
-    half_len = all_ref.shape[1] // (2 * n_dev)
-    head_dim = wq_buf.shape[2]
-    num_heads = q_ref.shape[1]
-    q_shape = (q_ref.shape[0], half_len, head_dim)
+    me = chip * 2 + core
+    n_seq, seq_len, kv_width = kv_scr.shape
+    half_len = seq_len // (2 * n_dev)
+    n_groups, rows, head_dim = q_scr.shape
+    num_heads = rows // half_len
+    key_len = 2 * half_len
+    scale = LOG2_E * head_dim ** -0.5
 
     def weights(head, slot):
         cols = pl.ds(pl.multiple_of(head * head_dim, head_dim), head_dim)
         return (pltpu.make_async_copy(wq_ref.at[:, cols], wq_buf.at[slot], w_sems.at[0, slot]),
                 pltpu.make_async_copy(wo_ref.at[cols, :], wo_buf.at[slot], w_sems.at[1, slot]))
 
+    loads = [pltpu.make_async_copy(h_ref, h_scr, load_sems.at[0]), pltpu.make_async_copy(dy_ref, dy_scr, load_sems.at[1])]
+    for load in loads:
+        load.start()
     for copy in weights(0, 0):
         copy.start()
     entry_barrier(peers + (partner,))
@@ -183,17 +195,21 @@
         return pl.ds(pl.multiple_of(piece * half_len, half_len), half_len)
 
     def place(step, way, seq):
-        return all_ref.at[seq, piece_rows(owner_at(chip, step, way, n_chip) * 2 + core, way)]
+        return kv_scr.at[seq, piece_rows(owner_at(chip, step, way, n_chip) * 2 + core, way)]
 
     def own(way, seq):
         return kv_ref.at[pl.ds((2 * seq + way) * half_len, half_len)]
 
     ring = RingGather(n_chip, peers, partner, own, place, n_seq, send_sems, recv_sems, mate_send, mate_recv)
     ring.first()
-    me = chip * 2 + core
     for seq in range(n_seq):
         for way in range(2):
-            all_ref[seq, piece_rows(me, way), :] = kv_ref[(2 * seq + way) * half_len:(2 * seq + way + 1) * half_len, :]
+            kv_scr[seq, piece_rows(me, way), :] = kv_ref[(2 * seq + way) * half_len:(2 * seq + way + 1) * half_len, :]
+    max_scr[...] = jnp.full_like(max_scr, NEG_BIG)
+    sum_scr[...] = jnp.zeros_like(sum_scr)
+    acc_scr[...] = jnp.zeros_like(acc_scr)
+    for load in loads:
+        load.wait()
 
     def project(head, slot):
         @pl.when(head < num_heads)
@@ -206,71 +222,102 @@
                 for copy in weights(head + 1, 1 - slot):
                     copy.start()
 
-            q_lin = dot(h_ref[...], wq_buf[slot], NN)
-            q_ref[:, head] = rotate(q_lin, cos_ref[...], sin_ref[...]).astype(jnp.bfloat16).reshape(q_shape)
-            da_ref[:, head] = dot(dy_ref[...], wo_buf[slot], NT).astype(jnp.bfloat16).reshape(q_shape)
-
-    project(0, 0)
+            head_rows = pl.ds(pl.multiple_of(head * half_len, half_len), half_len)
+            q_new = rotate(dot(h_scr[...], wq_buf[slot], NN), cos_ref[...], sin_ref[...]).astype(jnp.bfloat16)
+            da_new = dot(dy_scr[...], wo_buf[slot], NT).astype(jnp.bfloat16)
+            for group in range(n_groups):
+                q_scr[group, head_rows, :] = q_new[group * half_len:(group + 1) * half_len, :]
+                da_scr[group, head_rows, :] = da_new[group * half_len:(group + 1) * half_len, :]
+
+    def block(seq, group, start, masked):
+        index = 2 * seq + group
+        keys = pl.ds(pl.multiple_of(start, half_len), key_len)
+        scores = dot(kv_scr[seq, keys, :head_dim], qt_scr[index], NN) * scale
+        if masked:
+            piece = me if group == 0 else 2 * n_dev - 1 - me
+            scores = jnp.where(causal_mask(scores.shape, start, piece * half_len, half_len), scores, NEG_BIG)
+        old_max = max_scr[index]
+        new_max = jnp.maximum(old_max, jnp.max(scores, axis=0, keepdims=True))
+        rescale = jnp.exp2(old_max - new_max)
+        probs = jnp.exp2(scores - new_max)
+        max_scr[index] = new_max
+        sum_scr[index] = sum_scr[index] * rescale + jnp.sum(probs, axis=0, keepdims=True)
+        acc_scr[index] = acc_scr[index] * rescale + dot(kv_scr[seq, keys, head_dim:], probs.astype(jnp.bfloat16), TN)
+
+    def arrived(step, seq, masked):
+        for way in range(2):
+            ring.across(step, way, seq).wait_recv()
+        front = owner_at(chip, step, 0, n_chip)
+        back = owner_at(chip, step, 1, n_chip)
+        front_start = front * key_len
+        back_start = (n_dev - 1 - back) * key_len
+
+        @pl.when(step <= chip)
+        def _():
+            block(seq, 0, front_start, masked)
+
+        block(seq, 1, front_start, False)
+
+        @pl.when(chip + step < n_chip)
+        def _():
+            block(seq, 1, back_start, masked)
+
+    def attend(step, _):
+        lax.fori_loop(0, n_seq, lambda seq, _: arrived(step, seq, False), None)
+
+    def project_two(step):
+        lax.fori_loop(2 * step, 2 * step + 2, lambda head, _: project(head, lax.rem(head, 2)), None)
+
+    project_two(0)
     ring.middle(1)
 
-    def body(step, _):
-        project(step - 1, lax.rem(step - 1, 2))
+    def projecting(step, _):
+        project_two(step)
+        ring.middle(step + 1)
+
+    lax.fori_loop(1, 3, projecting, None)
+    lax.fori_loop(6, max(num_heads, 6), lambda head, _: project(head, lax.rem(head, 2)), None)
+    for group in range(n_groups):
+        qt_scr[group] = q_scr[group].T
+    ring.middle(4)
+    saves = [pltpu.make_async_copy(q_scr, q_ref, out_sems.at[0]), pltpu.make_async_copy(da_scr, da_ref, out_sems.at[1])]
+    for save in saves:
+        save.start()
+    lax.fori_loop(0, n_seq, lambda seq, _: arrived(0, seq, True), None)
+
+    def more(step, _):
         ring.middle(step)
-
-    lax.fori_loop(2, n_chip - 1, body, None)
-    project(n_chip - 2, (n_chip - 2) % 2)
+        lax.fori_loop(2 * step - 9, 2 * step - 7, attend, None)
+
+    lax.fori_loop(5, n_chip - 1, more, None)
     ring.last()
-    project(n_chip - 1, (n_chip - 1) % 2)
-    ring.drain()
-
-
-def causal_mask(shape, key_start, query_start, half_len):
-    key_idx = key_start + lax.broadcasted_iota(jnp.int32, shape, 0)
-    query_idx = query_start + lax.rem(lax.broadcasted_iota(jnp.int32, shape, 1), half_len)
-    return key_idx <= query_idx
-
-
-def attend_kernel(n_dev, q_ref, kv_ref, da_ref, a_ref, lse_ref, delta_ref, acc_scr, max_scr, sum_scr):
-    rows, head_dim = q_ref.shape[1:]
-    half_len = kv_ref.shape[1] // (2 * n_dev)
-    num_heads = rows // half_len
-    key_len = PIECES_PER_BLOCK * half_len
-    scale = LOG2_E * head_dim ** -0.5
-    me = lax.axis_index('cp')
-    for group in range(2):
-        piece = me if group == 0 else 2 * n_dev - 1 - me
-        last = lax.div(piece, PIECES_PER_BLOCK)
-        max_scr[...] = jnp.full_like(max_scr, NEG_BIG)
-        sum_scr[...] = jnp.zeros_like(sum_scr)
-        acc_scr[...] = jnp.zeros_like(acc_scr)
-
-        def block(step, masked, group=group, piece=piece):
-            start = pl.multiple_of(step * key_len, key_len)
-            keys = pl.ds(start, key_len)
-            scores = dot(kv_ref[0, keys, :head_dim], q_ref[group], NT) * scale
-            if masked:
-                scores = jnp.where(causal_mask(scores.shape, start, piece * half_len, half_len), scores, NEG_BIG)
-            old_max = max_scr[...]
-            new_max = jnp.maximum(old_max, jnp.max(scores, axis=0, keepdims=True))
-            rescale = jnp.exp2(old_max - new_max)
-            probs = jnp.exp2(scores - new_max)
-            max_scr[...] = new_max
-            sum_scr[...] = sum_scr[...] * rescale + jnp.sum(probs, axis=0, keepdims=True)
-            acc_scr[...] = acc_scr[...] * rescale + dot(kv_ref[0, keys, head_dim:], probs.astype(jnp.bfloat16), TN)
-
-        lax.fori_loop(0, last, lambda step, _: block(step, False), None)
-        block(last, True)
-        attn = (acc_scr[...] / sum_scr[...]).T.astype(jnp.bfloat16)
-        lse_ref[group] = max_scr[...] + jnp.log2(sum_scr[...])
-        prod = attn.astype(jnp.float32) * da_ref[group].astype(jnp.float32)
+    lax.fori_loop(2 * n_chip - 11, n_chip, attend, None)
+    for sub, way in ring.each:
+        ring.across(n_chip - 1, way, sub).wait_send()
+    saves.append(pltpu.make_async_copy(kv_scr, all_ref, out_sems.at[2]))
+    saves[2].start()
+
+    def finish(index, _):
+        attn = (acc_scr[index] / sum_scr[index]).T.astype(jnp.bfloat16)
+        lse_ref[index] = max_scr[index] + jnp.log2(sum_scr[index])
+        prod = attn.astype(jnp.float32) * da_scr[index].astype(jnp.float32)
         prod = prod[:, :head_dim // 2] + prod[:, head_dim // 2:]
-        delta_ref[group] = jnp.sum(prod.T, axis=0, keepdims=True)
+        delta_ref[index] = jnp.sum(prod.T, axis=0, keepdims=True)
+        out_rows = pl.ds(pl.multiple_of(index * half_len, half_len), half_len)
         for head in range(num_heads):
-            a_ref[group, :, head * head_dim:(head + 1) * head_dim] = attn[head * half_len:(head + 1) * half_len, :]
+            a_scr[out_rows, head * head_dim:(head + 1) * head_dim] = attn[head * half_len:(head + 1) * half_len, :]
+        pltpu.make_async_copy(a_scr.at[out_rows], a_ref.at[out_rows], out_sems.at[3 + index]).start()
+
+    lax.fori_loop(0, n_groups, finish, None)
+    for index in range(n_groups):
+        out_rows = pl.ds(index * half_len, half_len)
+        pltpu.make_async_copy(a_scr.at[out_rows], a_ref.at[out_rows], out_sems.at[3 + index]).wait()
+    for save in saves:
+        save.wait()
 
 
 def attend_grad_kernel(n_dev, q_ref, kv_ref, da_ref, lse_ref, delta_ref, cos_ref, sin_ref, a_ref, dy_ref, z_ref, wo_ref,
-                       q_scr, da_scr, kv_scr, dq_scr, dkv_scr, mate_scr, kv_local, kv_slots, a_scr, dy_scr, wo_local, wo_slots,
+                       q_scr, da_scr, kv_scr, qt_scr, dat_scr, dq_scr, dkv_scr, mate_scr, kv_local, kv_slots, a_scr, dy_scr, wo_local, wo_slots,
                        load_sems, swap_send, swap_recv, kv_send, kv_recv, mate_send, mate_recv, wo_send, wo_recv):
     n_chip, chip, core, peers, partner = ring_place(n_dev)
     me = chip * 2 + core
@@ -343,15 +390,17 @@
             piece = me + group * (2 * n_dev - 1 - 2 * me)
             last = lax.div(piece, PIECES_PER_BLOCK)
             dq_scr[...] = jnp.zeros_like(dq_scr)
+            qt_scr[...] = q_scr[index].T
+            dat_scr[...] = da_scr[index].T
 
             def block(step, masked):
                 start = pl.multiple_of(step * key_len, key_len)
                 keys = pl.ds(start, key_len)
                 k_blk, v_blk = kv_scr[seq, keys, :head_dim], kv_scr[seq, keys, head_dim:]
-                probs = jnp.exp2(dot(k_blk, q_scr[index], NT) * scale - lse_ref[index])
+                probs = jnp.exp2(dot(k_blk, qt_scr[...], NN) * scale - lse_ref[index])
                 if masked:
                     probs = jnp.where(causal_mask(probs.shape, start, piece * half_len, half_len), probs, 0.0)
-                d_scores = (probs * (dot(v_blk, da_scr[index], NT) - delta_ref[index])).astype(jnp.bfloat16)
+                d_scores = (probs * (dot(v_blk, dat_scr[...], NN) - delta_ref[index])).astype(jnp.bfloat16)
                 dq_scr[...] += dot(k_blk, d_scores, TN)
                 dkv_scr[seq, keys, :head_dim] += dot(d_scores, q_scr[index], NN) * head_dim ** -0.5
                 dkv_scr[seq, keys, head_dim:] += dot(probs.astype(jnp.bfloat16), da_scr[index], NN)
@@ -581,6 +630,25 @@
         gain_copy(offset).wait_send()
 
 
+def deliver_kernel(gz_ref, y_ref, dx_ref, wq_out, wk_out, wv_out, y_out, dx_out, gz_buf, in_sems, out_sems):
+    n_blk, blk_len, _ = gz_buf.shape
+    q_width, head_dim = wq_out.shape[1], wk_out.shape[1]
+    reads = [pltpu.make_async_copy(gz_ref.at[pl.ds(i * blk_len, blk_len)], gz_buf.at[i], in_sems.at[i]) for i in range(n_blk)]
+    for read in reads:
+        read.start()
+    writes = [pltpu.make_async_copy(src, out, out_sems.at[3 * n_blk + i]) for i, (src, out) in enumerate([(y_ref, y_out), (dx_ref, dx_out)])]
+    for write in writes:
+        write.start()
+    for i in range(n_blk):
+        reads[i].wait()
+        rows = pl.ds(i * blk_len, blk_len)
+        for j, (out, first) in enumerate([(wq_out, 0), (wk_out, q_width), (wv_out, q_width + head_dim)]):
+            writes.append(pltpu.make_async_copy(gz_buf.at[i, :, pl.ds(first, out.shape[1])], out.at[rows], out_sems.at[3 * i + j]))
+            writes[-1].start()
+    for write in writes:
+        write.wait()
+
+
 def solution(mesh):
     n_dev = mesh.shape['cp']
     n_chip, n_sub = n_dev // 2, 2
@@ -619,31 +687,20 @@
             compiler_params=params, name='norm_kv',
         )(x_flat, gain_row, w_key, w_value, cos_t, sin_t)
 
-        kv_all, q_heads, da_heads = pl.pallas_call(
-            functools.partial(gather_heads_kernel, n_dev),
-            in_specs=[vmem, vmem, vmem, hbm, hbm, vmem, vmem],
-            out_specs=[vmem, vmem, vmem],
-            out_shape=(shape(n_seq, seq_len, kv_width), shape(n_groups, num_heads, half_len, head_dim), shape(n_groups, num_heads, half_len, head_dim)),
-            scratch_shapes=[pltpu.VMEM((2, model_dim, head_dim), bf16), pltpu.VMEM((2, head_dim, model_dim), bf16), dma((2, 2))] + gather_sems(),
-            compiler_params=comm(0), name='gather_heads',
-        )(h_flat, dy_flat, kv_flat, w_query, w_out, cos_t, sin_t)
-        q_rows = q_heads.reshape(n_groups, rows, head_dim)
-        da_rows = da_heads.reshape(n_groups, rows, head_dim)
-
-        q_spec = pl.BlockSpec((2, rows, head_dim), lambda s: (s, 0, 0))
-        kv_spec = pl.BlockSpec((1, seq_len, kv_width), lambda s: (s, 0, 0))
-        tok_spec = pl.BlockSpec((2, half_len, q_width), lambda s: (s, 0, 0))
-        stat_spec = pl.BlockSpec((2, 1, rows), lambda s: (s, 0, 0))
-        attn, lse, delta = pl.pallas_call(
-            functools.partial(attend_kernel, n_dev),
-            grid=(n_seq,),
-            in_specs=[q_spec, kv_spec, q_spec],
-            out_specs=[tok_spec, stat_spec, stat_spec],
-            out_shape=(shape(n_groups, half_len, q_width), shape(n_groups, 1, rows, dtype=f32), shape(n_groups, 1, rows, dtype=f32)),
-            scratch_shapes=[pltpu.VMEM((head_dim, rows), f32), pltpu.VMEM((1, rows), f32), pltpu.VMEM((1, rows), f32)],
-            compiler_params=params, name='attend',
-        )(q_rows, kv_all, da_rows)
-        attn_flat = attn.reshape(n_rows, q_width)
+        groups = (n_groups, rows, head_dim)
+        kv_all, q_rows, da_rows, attn_flat, lse, delta = pl.pallas_call(
+            functools.partial(forward_kernel, n_dev),
+            in_specs=[vmem, vmem, vmem, hbm, hbm, hbm, hbm],
+            out_specs=[hbm, hbm, hbm, hbm, vmem, vmem],
+            out_shape=(shape(n_seq, seq_len, kv_width), shape(*groups), shape(*groups), shape(n_rows, q_width),
+                       shape(n_groups, 1, rows, dtype=f32), shape(n_groups, 1, rows, dtype=f32)),
+            scratch_shapes=[pltpu.VMEM((n_rows, model_dim), bf16), pltpu.VMEM((n_rows, model_dim), bf16), pltpu.VMEM((n_seq, seq_len, kv_width), bf16),
+                            pltpu.VMEM(groups, bf16), pltpu.VMEM(groups, bf16), pltpu.VMEM((n_groups, head_dim, rows), bf16), pltpu.VMEM((n_rows, q_width), bf16),
+                            pltpu.VMEM((n_groups, head_dim, rows), f32), pltpu.VMEM((n_groups, 1, rows), f32), pltpu.VMEM((n_groups, 1, rows), f32),
+                            pltpu.VMEM((2, model_dim, head_dim), bf16), pltpu.VMEM((2, head_dim, model_dim), bf16),
+                            dma((2,)), dma((3 + n_groups,)), dma((2, 2))] + gather_sems(),
+            compiler_params=comm(0), name='forward',
+        )(kv_flat, cos_t, sin_t, h_flat, dy_flat, w_query, w_out)
 
         z_width = q_width + kv_width
         wo_cols, wo_sub = model_dim // 2, q_width // (2 * n_chip * n_sub)
@@ -653,7 +710,7 @@
             out_specs=[vmem, vmem],
             out_shape=(shape(n_rows, z_width), shape(2, n_sub, wo_sub, wo_cols, dtype=f32)),
             scratch_shapes=[pltpu.VMEM((n_groups, rows, head_dim), bf16), pltpu.VMEM((n_groups, rows, head_dim), bf16),
-                            pltpu.VMEM((n_seq, seq_len, kv_width), bf16), pltpu.VMEM((head_dim, rows), f32),
+                            pltpu.VMEM((n_seq, seq_len, kv_width), bf16), pltpu.VMEM((head_dim, rows), bf16), pltpu.VMEM((head_dim, rows), bf16), pltpu.VMEM((head_dim, rows), f32),
                             pltpu.VMEM((n_seq, seq_len, kv_width), f32), pltpu.VMEM((2, n_chip, 2, half_len, kv_width), f32),
                             pltpu.VMEM((2, 2, half_len, kv_width), f32), pltpu.VMEM((2, n_chip - 1, 2, half_len, kv_width), f32),
                             pltpu.VMEM((2 * n_rows, q_width), bf16), pltpu.VMEM((2 * n_rows, wo_cols), bf16),
@@ -668,7 +725,7 @@
         grad_z, grad_wo, out_y, grad_x, grad_gain = pl.pallas_call(
             functools.partial(finish_kernel, n_dev),
             in_specs=[hbm] * 6 + [vmem, hbm, hbm, vmem, vmem],
-            out_specs=[hbm, hbm, vmem, vmem, vmem],
+            out_specs=[pl.BlockSpec(memory_space=pltpu.HBM), hbm, vmem, vmem, vmem],
             out_shape=(shape(model_dim, z_width, dtype=f32), shape(q_width, model_dim, dtype=f32), shape(n_rows, model_dim), shape(n_rows, model_dim),
                        shape(1, model_dim, dtype=f32)),
             scratch_shapes=[pltpu.VMEM((2 * n_rows, model_dim), bf16), pltpu.VMEM((2 * n_rows, core_width), bf16), pltpu.VMEM((n_rows, z_width), bf16),
@@ -680,7 +737,17 @@
             + gather_sems() + gather_sems() + [dma((2, 2, n_sub)), dma((n_dev,)), dma((n_dev,))],
             compiler_params=comm(2), name='finish',
         )(h_flat, z_flat, wo_part, attn_flat, x_flat, dy_flat, gain_row, w_query, w_out, w_key, w_value)
-        grad_wq, grad_wk, grad_wv = grad_z[:, :q_width], grad_z[:, q_width:q_width + head_dim], grad_z[:, q_width + head_dim:]
+        n_blk = n_dev
+        fixed = pl.BlockSpec(memory_space=pltpu.HBM)
+        grad_wq, grad_wk, grad_wv, out_y, grad_x = pl.pallas_call(
+            deliver_kernel,
+            in_specs=[fixed, vmem, vmem],
+            out_specs=[fixed] * 5,
+            out_shape=(shape(model_dim, q_width, dtype=f32), shape(model_dim, head_dim, dtype=f32), shape(model_dim, head_dim, dtype=f32),
+                       shape(n_rows, model_dim), shape(n_rows, model_dim)),
+            scratch_shapes=[pltpu.VMEM((n_blk, model_dim // n_blk, z_width), f32), dma((n_blk,)), dma((3 * n_blk + 2,))],
+            compiler_params=pltpu.CompilerParams(vmem_limit_bytes=40 * 1024 * 1024), name='deliver',
+        )(grad_z, out_y, grad_x)
         return out_y.reshape(tokens.shape), grad_x.reshape(tokens.shape), grad_wq, grad_wk, grad_wv, grad_wo, grad_gain.reshape(model_dim)
 
     seq_spec = P('dp', 'cp', None)

time: 555 us -> 542 us (0.977)
  local copies, waits for them, and re-layouts: 29.1 us -> 13.7 us
    slice x2 -> x0, local copies, waits for them, and re-layouts: 18.2 us -> none  [the longest x1 13.5 us: local_fn(): grad_z[:, :q_width]]
    unnamed x18 -> x10, local copies, waits for them, and re-layouts: 10.8 us -> 13.6 us
where the time goes in v2:
time: 542 us
  Pallas kernels  525 us (97%)
  local copies, waits for them, and re-layouts  13.7 us (3%)
    pallas_call x1, Pallas kernels, local_fn(): pl.pallas_call(functools.partial(finish_kernel, n_dev), in_specs=[hbm] *...  293 us
    pallas_call x1, Pallas kernels, local_fn(): pl.pallas_call(functools.partial(attend_grad_kernel, n_dev), in_specs=[hb...  157 us
    pallas_call x1, Pallas kernels, local_fn(): pl.pallas_call(functools.partial(forward_kernel, n_dev), in_specs=[vmem,...  54.7 us
    pallas_call x1, Pallas kernels, local_fn(): pl.pallas_call(deliver_kernel, in_specs=[fixed, vmem, vmem], out_specs=[f...  16.3 us
    unnamed x10, local copies, waits for them, and re-layouts  13.6 us

profile of v2, /device:TPU:21, one launch (start us, length us, event | category | flops | bytes accessed | tf_op | source)
XLA Modules:
  0.0 541.5 jit_solution(3369677875674888470)
XLA Ops:
  0.6 0.7 convert_element_type.10
  1.3 0.1 convert_element_type.11
  1.4 1.5 multiply_sine_fusion
  2.9 4.6 norm_kv.1
  7.6 54.7 %forward.1 = (bf16[2,3072,512]{2,1,0:T(8,128)(2,1)}, bf16[4,768,256]{2,1,0:T(8,128)(2,1)}, bf16[4,768,256]{2,1,0:T(8,128)(2,1)}, bf16[384,2048]{1,0:T(8,128)(2,1...) custom-call(bf16[384,512]{1,0:T(8,128)(2,1)} %get-tuple-element.28.kv_ref, f32[384,128]{1,0:T(8,128)} %get-tuple-element.48.cos_ref, ...), custom_call_target="tpu_custom_call" | custom-call | tf_op jit(solution)/shard_map/forward/pallas_call | solution.py:691
  62.2 156.8 %attend_grad.1 = (bf16[384,2560]{1,0:T(8,128)(2,1)}, f32[2,2,64,1024]{3,2,1,0:T(8,128)}) custom-call(bf16[4,768,256]{2,1,0:T(8,128)(2,1)} %get-tuple-element.29.q_ref, bf16[2,3072,512]{2,1,0:T(8,128)(2,1)} %get-tuple-element.30.kv_ref, bf16[4,768,256]{2,1,0:T(8,128)(2,1)} %get-tuple-element.31.da_ref, f32[4,1,768]{2,1,0:T(1,128)} %get-tuple-element.32.lse_ref, ...), custom_call_target="tpu_custom_call" | custom-call | tf_op jit(solution)/shard_map/attend_grad/pallas_call | solution.py:707
  219.0 292.6 %finish.1 = (f32[2048,2560]{1,0:T(8,128)}, f32[2048,2048]{1,0:T(8,128)}, bf16[384,2048]{1,0:T(8,128)(2,1)}, bf16[384,2048]{1,0:T(8,128)(2,1)}, f32[1,2048]{1,0:T(1,128)}) custom-call(bf16[384,2048]{1,0:T(8,128)(2,1)} %get-tuple-element.27.h_ref, bf16[384,2560]{1,0:T(8,128)(2,1)} %get-tuple-element.35.z_ref, ...), custom_call_target="tpu_custom_call" | custom-call | tf_op jit(solution)/shard_map/finish/pallas_call | solution.py:725
  511.6 0.0 copy-start
  511.7 1.4 copy-done
  513.1 0.0 copy-start.1
  513.1 1.4 copy-done.1
  514.5 0.0 copy-start.2
  514.5 16.3 %deliver.1 = (f32[2048,2048]{1,0:T(8,128)}, f32[2048,256]{1,0:T(8,128)}, f32[2048,256]{1,0:T(8,128)}, bf16[384,2048]{1,0:T(8,128)(2,1)}, bf16[384,2048]{1,0:T(8,128)(2,1)}) custom-call(f32[2048,2560]{1,0:T(8,128)} %get-tuple-element.37.gz_ref, bf16[384,2048]{1,0:T(8,128)(2,1)S(1)} %copy-done, bf16[384,2048]{1,0:T(8,128)(2,1)S(1)} %copy-done.1), custom_call_target="tpu_custom_call" | custom-call | tf_op jit(solution)/shard_map/deliver/pallas_call | solution.py:742
  530.7 4.0 copy-done.2
  534.8 0.0 copy-start.3
  534.8 6.2 %copy.17 = f32[2048,2048]{1,0:T(8,128)} copy(f32[2048,2048]{1,0:T(8,128)S(1)} %copy-done.2) | data formatting | bytes 33554432
  540.9 0.0 copy-done.3
  540.9 0.6 copy.18
  (1 shorter events, 0.0 us)
Async XLA Ops:
  511.6 1.4 copy-start
  513.1 1.4 copy-start.1
  514.5 20.3 %copy-start.2 = (f32[2048,2048]{1,0:T(8,128)S(1)}, f32[2048,2048]{1,0:T(8,128)}, u32[]{:S(2)}) copy-start(f32[2048,2048]{1,0:T(8,128)} %get-tuple-element.61) | copy-start | bytes 50331652
  534.8 6.2 %copy-start.3 = (f32[1,2048]{1,0:T(1,128)S(1)}, f32[1,2048]{1,0:T(1,128)}, u32[]{:S(2)}) copy-start(f32[1,2048]{1,0:T(1,128)} %get-tuple-element.46) | copy-start | bytes 24580

commit v3 on v2

--- a/solution.py
+++ b/solution.py
@@ -97,18 +97,24 @@
         for sub, way in self.each:
             self.hop(0, way, sub, True).start()
 
-    def middle(self, step, last=False):
-        for sub, way in self.each:
-            self.hop(step - 1, way, sub, isinstance(step, int) and step == 1).wait_send()
+    def middle(self, step, on_sum=None):
+        after_first = isinstance(step, int) and step == 1
+        if after_first:
+            for sub, way in self.each:
+                self.hop(0, way, sub, True).wait_send()
         self.make_local(step)
         for sub, way in self.each:
-            self.hop(step - 1, way, sub, isinstance(step, int) and step == 1).wait_recv()
+            self.hop(step - 1, way, sub, after_first).wait_recv()
             self.slots[way, step - 1, sub] = self.slots[way, step - 1, sub] + self.local_scr[way, sub]
-            if not last:
+            if not after_first:
+                self.hop(step - 1, way, sub).wait_send()
+            if on_sum is None:
                 self.hop(step, way, sub).start()
-
-    def last(self):
-        self.middle(self.n_chip - 1, True)
+            else:
+                on_sum(way, sub)
+
+    def last(self, on_sum):
+        self.middle(self.n_chip - 1, on_sum)
 
 
 class RingGather:
@@ -125,10 +131,13 @@
         src = self.own(way, sub) if first else self.place(step, way, sub)
         return remote(src, self.place(step, way, sub), self.mate_send.at[way, sub], self.mate_recv.at[way, step, sub], self.partner)
 
+    def start_first(self, way, sub):
+        self.onward(0, way, sub, True).start()
+        self.across(0, way, sub, True).start()
+
     def first(self):
         for sub, way in self.each:
-            self.onward(0, way, sub, True).start()
-            self.across(0, way, sub, True).start()
+            self.start_first(way, sub)
 
     def middle(self, step, last=False):
         after_first = isinstance(step, int) and step == 1
@@ -175,7 +184,6 @@
     half_len = seq_len // (2 * n_dev)
     n_groups, rows, head_dim = q_scr.shape
     num_heads = rows // half_len
-    key_len = 2 * half_len
     scale = LOG2_E * head_dim ** -0.5
 
     def weights(head, slot):
@@ -229,7 +237,7 @@
                 q_scr[group, head_rows, :] = q_new[group * half_len:(group + 1) * half_len, :]
                 da_scr[group, head_rows, :] = da_new[group * half_len:(group + 1) * half_len, :]
 
-    def block(seq, group, start, masked):
+    def block(seq, group, start, key_len, masked):
         index = 2 * seq + group
         keys = pl.ds(pl.multiple_of(start, half_len), key_len)
         scores = dot(kv_scr[seq, keys, :head_dim], qt_scr[index], NN) * scale
@@ -244,26 +252,41 @@
         sum_scr[index] = sum_scr[index] * rescale + jnp.sum(probs, axis=0, keepdims=True)
         acc_scr[index] = acc_scr[index] * rescale + dot(kv_scr[seq, keys, head_dim:], probs.astype(jnp.bfloat16), TN)
 
-    def arrived(step, seq, masked):
-        for way in range(2):
-            ring.across(step, way, seq).wait_recv()
-        front = owner_at(chip, step, 0, n_chip)
-        back = owner_at(chip, step, 1, n_chip)
-        front_start = front * key_len
-        back_start = (n_dev - 1 - back) * key_len
-
-        @pl.when(step <= chip)
-        def _():
-            block(seq, 0, front_start, masked)
-
-        block(seq, 1, front_start, False)
-
-        @pl.when(chip + step < n_chip)
-        def _():
-            block(seq, 1, back_start, masked)
-
-    def attend(step, _):
-        lax.fori_loop(0, n_seq, lambda seq, _: arrived(step, seq, False), None)
+    def attend_pair(pair, seq):
+        chip_len = 2 * half_len
+        for step in range(2):
+            for way in range(2):
+                ring.across(2 * pair + step, way, seq).wait_recv()
+        front = owner_at(chip, 2 * pair, 0, n_chip)
+        before = owner_at(chip, 2 * pair + 1, 0, n_chip)
+        back = chip + 2 * pair
+
+        @pl.when(front > 0)
+        def _():
+            block(seq, 1, before * chip_len, 2 * chip_len, False)
+
+        @pl.when(front == 0)
+        def _():
+            lax.fori_loop(0, 2, lambda i, _: block(seq, 1, (front + i * (before - front)) * chip_len, chip_len, False), None)
+
+        @pl.when(2 * pair < chip)
+        def _():
+            block(seq, 0, before * chip_len, 2 * chip_len, True)
+
+        @pl.when(2 * pair == chip)
+        def _():
+            block(seq, 0, front * chip_len, chip_len, True)
+
+        @pl.when(back + 1 < n_chip)
+        def _():
+            block(seq, 1, (n_dev - 2 - back) * chip_len, 2 * chip_len, True)
+
+        @pl.when(back + 1 == n_chip)
+        def _():
+            block(seq, 1, (n_dev - 1 - back) * chip_len, chip_len, True)
+
+    def attend(pair, _):
+        lax.fori_loop(0, n_seq, lambda seq, _: attend_pair(pair, seq), None)
 
     def project_two(step):
         lax.fori_loop(2 * step, 2 * step + 2, lambda head, _: project(head, lax.rem(head, 2)), None)
@@ -283,15 +306,19 @@
     saves = [pltpu.make_async_copy(q_scr, q_ref, out_sems.at[0]), pltpu.make_async_copy(da_scr, da_ref, out_sems.at[1])]
     for save in saves:
         save.start()
-    lax.fori_loop(0, n_seq, lambda seq, _: arrived(0, seq, True), None)
-
-    def more(step, _):
-        ring.middle(step)
-        lax.fori_loop(2 * step - 9, 2 * step - 7, attend, None)
-
-    lax.fori_loop(5, n_chip - 1, more, None)
-    ring.last()
-    lax.fori_loop(2 * n_chip - 11, n_chip, attend, None)
+
+    def pairs(pair, _):
+        attend(pair, None)
+
+        @pl.when(pair < n_chip - 6)
+        def _():
+            ring.middle(pair + 5)
+
+        @pl.when(pair == n_chip - 6)
+        def _():
+            ring.last()
+
+    lax.fori_loop(0, n_chip // 2, pairs, None)
     for sub, way in ring.each:
         ring.across(n_chip - 1, way, sub).wait_send()
     saves.append(pltpu.make_async_copy(kv_scr, all_ref, out_sems.at[2]))
@@ -438,19 +465,21 @@
         kv_ring.middle(step)
 
     lax.fori_loop(2, n_chip - 3, both, None)
-    wo_ring.last()
-    for way in range(2):
-        for sub in range(wo_local.shape[1]):
-            wo_ref[way, sub] = wo_slots[way, n_chip - 2, sub]
+
+    def keep_wo(way, sub):
+        wo_ref[way, sub] = wo_slots[way, n_chip - 2, sub]
+
+    wo_ring.last(keep_wo)
     kv_ring.middle(n_chip - 3)
     kv_ring.middle(n_chip - 2)
-    kv_ring.last()
-    for way in range(2):
-        for sub in range(2):
-            out_rows = slice((2 * way + sub) * half_len, (2 * way + sub + 1) * half_len)
-            total = kv_slots[way, n_chip - 2, sub]
-            z_ref[out_rows, q_width:q_width + head_dim] = rotate_back(total[:, :head_dim], cos_ref[out_rows, :], sin_ref[out_rows, :]).astype(jnp.bfloat16)
-            z_ref[out_rows, q_width + head_dim:] = total[:, head_dim:].astype(jnp.bfloat16)
+
+    def keep_kv(way, sub):
+        out_rows = slice((2 * way + sub) * half_len, (2 * way + sub + 1) * half_len)
+        total = kv_slots[way, n_chip - 2, sub]
+        z_ref[out_rows, q_width:q_width + head_dim] = rotate_back(total[:, :head_dim], cos_ref[out_rows, :], sin_ref[out_rows, :]).astype(jnp.bfloat16)
+        z_ref[out_rows, q_width + head_dim:] = total[:, head_dim:].astype(jnp.bfloat16)
+
+    kv_ring.last(keep_kv)
 
     def mates_sent(step, _):
         for way in range(2):
@@ -593,10 +622,12 @@
 
     lax.fori_loop(2, n_chip - 1, phase_one, None)
     wo_gather.last()
-    z_ring.last()
-    z_gather.first()
-    for keep in keeps[1]:
-        keep.start()
+
+    def pass_on(way, sub):
+        z_gather.start_first(way, sub)
+        keeps[1][2 * sub + way].start()
+
+    z_ring.last(pass_on)
     d_hidden(n_chip - 2, (n_chip - 2) % 2)
     d_hidden(n_chip - 1, (n_chip - 1) % 2)
     gain_slots[me] = jnp.zeros(gain_slots.shape[1:], jnp.float32)
@@ -630,20 +661,27 @@
         gain_copy(offset).wait_send()
 
 
-def deliver_kernel(gz_ref, y_ref, dx_ref, wq_out, wk_out, wv_out, y_out, dx_out, gz_buf, in_sems, out_sems):
-    n_blk, blk_len, _ = gz_buf.shape
+def deliver_kernel(gz_ref, gwo_ref, y_ref, dx_ref, wq_out, wk_out, wv_out, wo_out, y_out, dx_out, gz_buf, gwo_buf, y_buf, dx_buf, in_sems, out_sems):
+    n_blk, z_len, _ = gz_buf.shape
+    wo_len = gwo_buf.shape[1]
     q_width, head_dim = wq_out.shape[1], wk_out.shape[1]
-    reads = [pltpu.make_async_copy(gz_ref.at[pl.ds(i * blk_len, blk_len)], gz_buf.at[i], in_sems.at[i]) for i in range(n_blk)]
+    jobs = []
+    for i in range(n_blk):
+        rows = pl.ds(i * z_len, z_len)
+        parts = [(gz_buf.at[i, :, pl.ds(first, out.shape[1])], out.at[rows]) for out, first in ((wq_out, 0), (wk_out, q_width), (wv_out, q_width + head_dim))]
+        jobs.append((gz_ref.at[rows], gz_buf.at[i], parts))
+        rows = pl.ds(i * wo_len, wo_len)
+        jobs.append((gwo_ref.at[rows], gwo_buf.at[i], [(gwo_buf.at[i], wo_out.at[rows])]))
+    for src, buf, out in ((y_ref, y_buf, y_out), (dx_ref, dx_buf, dx_out)):
+        jobs.append((src, buf, [(buf, out)]))
+    reads = [pltpu.make_async_copy(src, buf, in_sems.at[i]) for i, (src, buf, _) in enumerate(jobs)]
     for read in reads:
         read.start()
-    writes = [pltpu.make_async_copy(src, out, out_sems.at[3 * n_blk + i]) for i, (src, out) in enumerate([(y_ref, y_out), (dx_ref, dx_out)])]
-    for write in writes:
-        write.start()
-    for i in range(n_blk):
-        reads[i].wait()
-        rows = pl.ds(i * blk_len, blk_len)
-        for j, (out, first) in enumerate([(wq_out, 0), (wk_out, q_width), (wv_out, q_width + head_dim)]):
-            writes.append(pltpu.make_async_copy(gz_buf.at[i, :, pl.ds(first, out.shape[1])], out.at[rows], out_sems.at[3 * i + j]))
+    writes = []
+    for read, (_, _, parts) in zip(reads, jobs):
+        read.wait()
+        for src, dst in parts:
+            writes.append(pltpu.make_async_copy(src, dst, out_sems.at[len(writes)]))
             writes[-1].start()
     for write in writes:
         write.wait()
@@ -738,16 +776,17 @@
             compiler_params=comm(2), name='finish',
         )(h_flat, z_flat, wo_part, attn_flat, x_flat, dy_flat, gain_row, w_query, w_out, w_key, w_value)
         n_blk = n_dev
-        fixed = pl.BlockSpec(memory_space=pltpu.HBM)
-        grad_wq, grad_wk, grad_wv, out_y, grad_x = pl.pallas_call(
+        grad_wq, grad_wk, grad_wv, grad_wo, out_y, grad_x = pl.pallas_call(
             deliver_kernel,
-            in_specs=[fixed, vmem, vmem],
-            out_specs=[fixed] * 5,
+            in_specs=[hbm] * 4,
+            out_specs=[hbm] * 6,
             out_shape=(shape(model_dim, q_width, dtype=f32), shape(model_dim, head_dim, dtype=f32), shape(model_dim, head_dim, dtype=f32),
-                       shape(n_rows, model_dim), shape(n_rows, model_dim)),
-            scratch_shapes=[pltpu.VMEM((n_blk, model_dim // n_blk, z_width), f32), dma((n_blk,)), dma((3 * n_blk + 2,))],
-            compiler_params=pltpu.CompilerParams(vmem_limit_bytes=40 * 1024 * 1024), name='deliver',
-        )(grad_z, out_y, grad_x)
+                       shape(q_width, model_dim, dtype=f32), shape(n_rows, model_dim), shape(n_rows, model_dim)),
+            scratch_shapes=[pltpu.VMEM((n_blk, model_dim // n_blk, z_width), f32), pltpu.VMEM((n_blk, q_width // n_blk, model_dim), f32),
+                            pltpu.VMEM((n_rows, model_dim), bf16), pltpu.VMEM((n_rows, model_dim), bf16),
+                            dma((2 * n_blk + 2,)), dma((4 * n_blk + 2,))],
+            compiler_params=params, name='deliver',
+        )(grad_z, grad_wo, out_y, grad_x)
         return out_y.reshape(tokens.shape), grad_x.reshape(tokens.shape), grad_wq, grad_wk, grad_wv, grad_wo, grad_gain.reshape(model_dim)
 
     seq_spec = P('dp', 'cp', None)

time: 542 us -> 535 us (0.987)
  local copies, waits for them, and re-layouts: 13.7 us -> 0.69 us
  Pallas kernels: 525 us -> 531 us
    unnamed x10 -> x3, local copies, waits for them, and re-layouts: 13.6 us -> 0.61 us
    pallas_call x1, Pallas kernels: 16.3 us -> 27.5 us  [local_fn(): pl.pallas_call(deliver_kernel, in_specs=[hbm] * 4, out_specs=[hbm] * 6, o...]
    pallas_call x1, Pallas kernels: 157 us -> 150 us  [local_fn(): pl.pallas_call(functools.partial(attend_grad_kernel, n_dev), in_specs=[hb...]
where the time goes in v3:
time: 535 us
  Pallas kernels  531 us (99%)
    pallas_call x1, Pallas kernels, local_fn(): pl.pallas_call(functools.partial(finish_kernel, n_dev), in_specs=[hbm] *...  292 us
    pallas_call x1, Pallas kernels, local_fn(): pl.pallas_call(functools.partial(attend_grad_kernel, n_dev), in_specs=[hb...  150 us
    pallas_call x1, Pallas kernels, local_fn(): pl.pallas_call(functools.partial(forward_kernel, n_dev), in_specs=[vmem,...  56.9 us
    pallas_call x1, Pallas kernels, local_fn(): pl.pallas_call(deliver_kernel, in_specs=[hbm] * 4, out_specs=[hbm] * 6, o...  27.5 us

profile of v3, /device:TPU:21, one launch (start us, length us, event | category | flops | bytes accessed | tf_op | source)
XLA Modules:
  0.0 534.9 jit_solution(13330834113954745702)
XLA Ops:
  0.6 0.7 convert_element_type.10
  1.3 0.1 convert_element_type.11
  1.4 1.5 multiply_sine_fusion
  2.9 4.6 norm_kv.1
  7.6 56.9 %forward.1 = (bf16[2,3072,512]{2,1,0:T(8,128)(2,1)}, bf16[4,768,256]{2,1,0:T(8,128)(2,1)}, bf16[4,768,256]{2,1,0:T(8,128)(2,1)}, bf16[384,2048]{1,0:T(8,128)(2,1...) custom-call(bf16[384,512]{1,0:T(8,128)(2,1)} %get-tuple-element.29.kv_ref, f32[384,128]{1,0:T(8,128)} %get-tuple-element.50.cos_ref, ...), custom_call_target="tpu_custom_call" | custom-call | tf_op jit(solution)/shard_map/forward/pallas_call | solution.py:729
  64.5 150.0 %attend_grad.1 = (bf16[384,2560]{1,0:T(8,128)(2,1)}, f32[2,2,64,1024]{3,2,1,0:T(8,128)}) custom-call(bf16[4,768,256]{2,1,0:T(8,128)(2,1)} %get-tuple-element.30.q_ref, bf16[2,3072,512]{2,1,0:T(8,128)(2,1)} %get-tuple-element.31.kv_ref, bf16[4,768,256]{2,1,0:T(8,128)(2,1)} %get-tuple-element.32.da_ref, f32[4,1,768]{2,1,0:T(1,128)} %get-tuple-element.33.lse_ref, ...), custom_call_target="tpu_custom_call" | custom-call | tf_op jit(solution)/shard_map/attend_grad/pallas_call | solution.py:745
  214.5 292.2 %finish.1 = (f32[2048,2560]{1,0:T(8,128)}, f32[2048,2048]{1,0:T(8,128)}, bf16[384,2048]{1,0:T(8,128)(2,1)}, bf16[384,2048]{1,0:T(8,128)(2,1)}, f32[1,2048]{1,0:T(1,128)}) custom-call(bf16[384,2048]{1,0:T(8,128)(2,1)} %get-tuple-element.28.h_ref, bf16[384,2560]{1,0:T(8,128)(2,1)} %get-tuple-element.36.z_ref, ...), custom_call_target="tpu_custom_call" | custom-call | tf_op jit(solution)/shard_map/finish/pallas_call | solution.py:763
  506.7 0.0 copy-start
  506.7 27.5 %deliver.1 = (f32[2048,2048]{1,0:T(8,128)}, f32[2048,256]{1,0:T(8,128)}, f32[2048,256]{1,0:T(8,128)}, f32[2048,2048]{1,0:T(8,128)}, bf16[384,2048]{1,0:T(8,128)(2,1)}, /*index=5*/bf16[384,2048]{1,0:T(8,128)(2,1)}) custom-call(f32[2048,2560]{1,0:T(8,128)} %get-tuple-element.38.gz_ref, f32[2048,2048]{1,0:T(8,128)} %get-tuple-element.39.gwo_ref, ...), custom_call_target="tpu_custom_call" | custom-call | tf_op jit(solution)/shard_map/deliver/pallas_call | solution.py:779
  534.3 0.0 copy-done
  534.3 0.6 copy.16
  (1 shorter events, 0.0 us)
Async XLA Ops:
  506.7 27.6 %copy-start = (f32[1,2048]{1,0:T(1,128)S(1)}, f32[1,2048]{1,0:T(1,128)}, u32[]{:S(2)}) copy-start(f32[1,2048]{1,0:T(1,128)} %get-tuple-element.48) | copy-start | bytes 24580

commit v4 on v3

--- a/solution.py
+++ b/solution.py
@@ -83,17 +83,31 @@
 
 
 class RingReduce:
-    def __init__(self, n_chip, peers, make_local, local_scr, slots, send_sems, recv_sems):
-        self.n_chip, self.peers, self.make_local = n_chip, peers, make_local
+    def __init__(self, n_chip, peers, make_local, local_scr, slots, send_sems, recv_sems, first_buf=None):
+        self.n_chip, self.peers, self.make_local, self.first_buf = n_chip, peers, make_local, first_buf
         self.local_scr, self.slots, self.send_sems, self.recv_sems = local_scr, slots, send_sems, recv_sems
         self.each = [(sub, way) for sub in range(slots.shape[2]) for way in range(2)]
 
     def hop(self, step, way, sub, first=False):
-        src = self.local_scr.at[way, sub] if first else self.slots.at[way, step - 1, sub]
+        buf = self.local_scr if self.first_buf is None else self.first_buf
+        src = buf.at[way, sub] if first else self.slots.at[way, step - 1, sub]
         return remote(src, self.slots.at[way, step, sub], self.send_sems.at[way, sub], self.recv_sems.at[way, step, sub], self.peers[way])
+
+    def arrival(self, step, way, sub):
+        slot = self.slots.at[way, step, sub]
+        return remote(slot, slot, self.send_sems.at[way, sub], self.recv_sems.at[way, step, sub], self.peers[way])
+
+    def serve(self, step, sub):
+        for way in range(2):
+            self.arrival(step - 1, way, sub).wait_recv()
+            self.slots[way, step - 1, sub] = self.slots[way, step - 1, sub] + self.local_scr[way, sub]
+            self.arrival(step - 1, way, sub).wait_send()
+            self.hop(step, way, sub).start()
 
     def first(self):
         self.make_local(0)
+        if self.first_buf is not None:
+            self.first_buf[...] = self.local_scr[...]
         for sub, way in self.each:
             self.hop(0, way, sub, True).start()
 
@@ -175,11 +189,12 @@
     return key_idx <= query_idx
 
 
-def forward_kernel(n_dev, kv_ref, cos_ref, sin_ref, h_ref, dy_ref, wq_ref, wo_ref, all_ref, q_ref, da_ref, a_ref, lse_ref, delta_ref,
+def forward_kernel(n_dev, kv_ref, cos_ref, sin_ref, h_ref, dy_ref, wq_ref, wo_ref, all_ref, q_ref, da_ref, a_ref, dyc_ref, lse_ref, delta_ref,
                    h_scr, dy_scr, kv_scr, q_scr, da_scr, qt_scr, a_scr, acc_scr, max_scr, sum_scr, wq_buf, wo_buf,
-                   load_sems, out_sems, w_sems, send_sems, recv_sems, mate_send, mate_recv):
+                   load_sems, out_sems, w_sems, swap_send, swap_recv, send_sems, recv_sems, mate_send, mate_recv):
     n_chip, chip, core, peers, partner = ring_place(n_dev)
     me = chip * 2 + core
+    n_rows, dy_cols = h_scr.shape[0], dyc_ref.shape[1]
     n_seq, seq_len, kv_width = kv_scr.shape
     half_len = seq_len // (2 * n_dev)
     n_groups, rows, head_dim = q_scr.shape
@@ -218,6 +233,14 @@
     acc_scr[...] = jnp.zeros_like(acc_scr)
     for load in loads:
         load.wait()
+
+    def half_cols(which):
+        return pl.ds(pl.multiple_of(which * dy_cols, dy_cols), dy_cols)
+
+    dy_keep = pltpu.make_async_copy(dy_scr.at[:, half_cols(core)], dyc_ref.at[pl.ds(0, n_rows)], load_sems.at[2])
+    dy_swap = remote(dy_scr.at[:, half_cols(1 - core)], dyc_ref.at[pl.ds(n_rows, n_rows)], swap_send.at[n_groups], swap_recv.at[n_groups], partner)
+    dy_keep.start()
+    dy_swap.start()
 
     def project(head, slot):
         @pl.when(head < num_heads)
@@ -285,9 +308,6 @@
         def _():
             block(seq, 1, (n_dev - 1 - back) * chip_len, chip_len, True)
 
-    def attend(pair, _):
-        lax.fori_loop(0, n_seq, lambda seq, _: attend_pair(pair, seq), None)
-
     def project_two(step):
         lax.fori_loop(2 * step, 2 * step + 2, lambda head, _: project(head, lax.rem(head, 2)), None)
 
@@ -307,18 +327,18 @@
     for save in saves:
         save.start()
 
-    def pairs(pair, _):
-        attend(pair, None)
-
-        @pl.when(pair < n_chip - 6)
-        def _():
-            ring.middle(pair + 5)
-
-        @pl.when(pair == n_chip - 6)
+    def attend(turn, _):
+        attend_pair(lax.div(turn, n_seq), lax.rem(turn, n_seq))
+
+        @pl.when(turn < n_chip - 6)
+        def _():
+            ring.middle(turn + 5)
+
+        @pl.when(turn == n_chip - 6)
         def _():
             ring.last()
 
-    lax.fori_loop(0, n_chip // 2, pairs, None)
+    lax.fori_loop(0, n_chip // 2 * n_seq, attend, None)
     for sub, way in ring.each:
         ring.across(n_chip - 1, way, sub).wait_send()
     saves.append(pltpu.make_async_copy(kv_scr, all_ref, out_sems.at[2]))
@@ -333,19 +353,31 @@
         out_rows = pl.ds(pl.multiple_of(index * half_len, half_len), half_len)
         for head in range(num_heads):
             a_scr[out_rows, head * head_dim:(head + 1) * head_dim] = attn[head * half_len:(head + 1) * half_len, :]
-        pltpu.make_async_copy(a_scr.at[out_rows], a_ref.at[out_rows], out_sems.at[3 + index]).start()
+        keep_group(index).start()
+        swap_group(index).start()
+
+    def keep_group(index):
+        out_rows = pl.ds(pl.multiple_of(index * half_len, half_len), half_len)
+        return pltpu.make_async_copy(a_scr.at[out_rows], a_ref.at[out_rows], out_sems.at[3 + index])
+
+    def swap_group(index):
+        out_rows = pl.ds(pl.multiple_of(index * half_len, half_len), half_len)
+        far_rows = pl.ds(pl.multiple_of(n_rows + index * half_len, half_len), half_len)
+        return remote(a_scr.at[out_rows], a_ref.at[far_rows], swap_send.at[index], swap_recv.at[index], partner)
 
     lax.fori_loop(0, n_groups, finish, None)
+    dy_keep.wait()
+    dy_swap.wait()
     for index in range(n_groups):
-        out_rows = pl.ds(index * half_len, half_len)
-        pltpu.make_async_copy(a_scr.at[out_rows], a_ref.at[out_rows], out_sems.at[3 + index]).wait()
+        keep_group(index).wait()
+        swap_group(index).wait()
     for save in saves:
         save.wait()
 
 
 def attend_grad_kernel(n_dev, q_ref, kv_ref, da_ref, lse_ref, delta_ref, cos_ref, sin_ref, a_ref, dy_ref, z_ref, wo_ref,
                        q_scr, da_scr, kv_scr, qt_scr, dat_scr, dq_scr, dkv_scr, mate_scr, kv_local, kv_slots, a_scr, dy_scr, wo_local, wo_slots,
-                       load_sems, swap_send, swap_recv, kv_send, kv_recv, mate_send, mate_recv, wo_send, wo_recv):
+                       load_sems, kv_send, kv_recv, mate_send, mate_recv, wo_send, wo_recv):
     n_chip, chip, core, peers, partner = ring_place(n_dev)
     me = chip * 2 + core
     rows, head_dim = q_scr.shape[1:]
@@ -353,18 +385,11 @@
     half_len = seq_len // (2 * n_dev)
     num_heads = rows // half_len
     q_width = num_heads * head_dim
-    n_rows = a_ref.shape[0]
     key_len = PIECES_PER_BLOCK * half_len
     scale = LOG2_E * head_dim ** -0.5
-    dy_cols = dy_scr.shape[1]
-    mine, other = pl.ds(0, n_rows), pl.ds(n_rows, n_rows)
-
-    def cols(which, size):
-        return pl.ds(pl.multiple_of(which * size, size), size)
-
     loads = [
-        pltpu.make_async_copy(a_ref, a_scr.at[mine], load_sems.at[0]),
-        pltpu.make_async_copy(dy_ref.at[:, cols(core, dy_cols)], dy_scr.at[mine], load_sems.at[1]),
+        pltpu.make_async_copy(a_ref, a_scr, load_sems.at[0]),
+        pltpu.make_async_copy(dy_ref, dy_scr, load_sems.at[1]),
         pltpu.make_async_copy(q_ref, q_scr, load_sems.at[2]),
         pltpu.make_async_copy(da_ref, da_scr, load_sems.at[3]),
         pltpu.make_async_copy(kv_ref, kv_scr, load_sems.at[4]),
@@ -372,17 +397,8 @@
     for load in loads:
         load.start()
     entry_barrier(peers + (partner,))
-    swaps = [
-        remote(a_ref, a_scr.at[other], swap_send.at[0], swap_recv.at[0], partner),
-        remote(dy_ref.at[:, cols(1 - core, dy_cols)], dy_scr.at[other], swap_send.at[1], swap_recv.at[1], partner),
-    ]
-    for swap in swaps:
-        swap.start()
-    dkv_scr[...] = jnp.zeros_like(dkv_scr)
     loads[0].wait()
     loads[1].wait()
-    for swap in swaps:
-        swap.wait_recv()
 
     def wo_local_term(step):
         n_sub, sub_len = wo_local.shape[1:3]
@@ -408,32 +424,37 @@
                 dev = chunk_at(chip, step, way, n_chip) * 2 + core
                 kv_local[way, sub] = dkv_scr[way, piece_rows(dev, sub), :] + mate_scr[way, step, sub]
 
-    wo_ring = RingReduce(n_chip, peers, wo_local_term, wo_local, wo_slots, wo_send, wo_recv)
+    wo_ring = RingReduce(n_chip, peers, wo_local_term, wo_local, wo_slots, wo_send, wo_recv, wo_ref)
     kv_ring = RingReduce(n_chip, peers, kv_local_term, kv_local, kv_slots, kv_send, kv_recv)
 
-    def attend_seq(seq):
-        def one_group(group, _):
-            index = 2 * seq + group
-            piece = me + group * (2 * n_dev - 1 - 2 * me)
-            last = lax.div(piece, PIECES_PER_BLOCK)
+    front_blocks = lax.div(me, PIECES_PER_BLOCK) + 1
+    all_blocks = 2 * n_dev // PIECES_PER_BLOCK + 1
+    chunk_blocks = 3
+
+    def block_of(seq, turn):
+        group = jnp.where(turn >= front_blocks, 1, 0)
+        step = turn - group * front_blocks
+        index = 2 * seq + group
+        piece = me + group * (2 * n_dev - 1 - 2 * me)
+        start = pl.multiple_of(step * key_len, key_len)
+        keys = pl.ds(start, key_len)
+
+        @pl.when(step == 0)
+        def _():
             dq_scr[...] = jnp.zeros_like(dq_scr)
             qt_scr[...] = q_scr[index].T
             dat_scr[...] = da_scr[index].T
 
-            def block(step, masked):
-                start = pl.multiple_of(step * key_len, key_len)
-                keys = pl.ds(start, key_len)
-                k_blk, v_blk = kv_scr[seq, keys, :head_dim], kv_scr[seq, keys, head_dim:]
-                probs = jnp.exp2(dot(k_blk, qt_scr[...], NN) * scale - lse_ref[index])
-                if masked:
-                    probs = jnp.where(causal_mask(probs.shape, start, piece * half_len, half_len), probs, 0.0)
-                d_scores = (probs * (dot(v_blk, dat_scr[...], NN) - delta_ref[index])).astype(jnp.bfloat16)
-                dq_scr[...] += dot(k_blk, d_scores, TN)
-                dkv_scr[seq, keys, :head_dim] += dot(d_scores, q_scr[index], NN) * head_dim ** -0.5
-                dkv_scr[seq, keys, head_dim:] += dot(probs.astype(jnp.bfloat16), da_scr[index], NN)
-
-            lax.fori_loop(0, last, lambda step, _: block(step, False), None)
-            block(last, True)
+        k_blk, v_blk = kv_scr[seq, keys, :head_dim], kv_scr[seq, keys, head_dim:]
+        probs = jnp.exp2(dot(k_blk, qt_scr[...], NN) * scale - lse_ref[index])
+        probs = jnp.where(causal_mask(probs.shape, start, piece * half_len, half_len), probs, 0.0)
+        d_scores = (probs * (dot(v_blk, dat_scr[...], NN) - delta_ref[index])).astype(jnp.bfloat16)
+        dq_scr[...] += dot(k_blk, d_scores, TN)
+        dkv_scr[seq, keys, :head_dim] += dot(d_scores, q_scr[index], NN) * head_dim ** -0.5
+        dkv_scr[seq, keys, head_dim:] += dot(probs.astype(jnp.bfloat16), da_scr[index], NN)
+
+        @pl.when(step == lax.div(piece, PIECES_PER_BLOCK))
+        def _():
             dq = dq_scr[...].T * head_dim ** -0.5
             out_rows = pl.ds(pl.multiple_of(index * half_len, half_len), half_len)
             cos_t, sin_t = cos_ref[out_rows, :], sin_ref[out_rows, :]
@@ -441,37 +462,48 @@
                 dq_head = dq[head * half_len:(head + 1) * half_len, :]
                 z_ref[out_rows, head * head_dim:(head + 1) * head_dim] = rotate_back(dq_head, cos_t, sin_t).astype(jnp.bfloat16)
 
-        lax.fori_loop(0, 2, one_group, None)
-
-        def send_mate(step, _):
-            for sub in range(2):
-                mate_copy(step, seq, sub).start()
-
-        lax.fori_loop(0, n_chip, send_mate, None)
+    n_chunks = all_blocks // chunk_blocks
+
+    def chunk(turn, _):
+        seq, part = lax.div(turn, n_chunks), lax.rem(turn, n_chunks)
+        lax.fori_loop(part * chunk_blocks, (part + 1) * chunk_blocks, lambda at, _: block_of(seq, at), None)
+        for way in range(n_seq):
+            @pl.when(turn == (way + 1) * n_chunks - 1)
+            def _():
+                def send_mate(step, _):
+                    for sub in range(2):
+                        mate_copy(step, way, sub).start()
+
+                lax.fori_loop(0, n_chip, send_mate, None)
+
+        step, sub = lax.div(turn, 2) + 1, lax.rem(turn, 2)
+
+        @pl.when(sub == 0)
+        def _():
+            wo_local_term(step)
+
+        wo_ring.serve(step, sub)
 
     wo_ring.first()
+    dkv_scr[...] = jnp.zeros_like(dkv_scr)
     for load in loads[2:]:
         load.wait()
-    attend_seq(0)
-    wo_ring.middle(1)
-    attend_seq(1)
-    wo_ring.middle(2)
+    lax.fori_loop(0, n_seq * n_chunks, chunk, None)
     kv_ring.first()
-    wo_ring.middle(3)
+    wo_ring.middle(4)
     kv_ring.middle(1)
 
     def both(step, _):
-        wo_ring.middle(step + 2)
+        wo_ring.middle(step + 3)
         kv_ring.middle(step)
 
-    lax.fori_loop(2, n_chip - 3, both, None)
+    lax.fori_loop(2, n_chip - 4, both, None)
 
     def keep_wo(way, sub):
         wo_ref[way, sub] = wo_slots[way, n_chip - 2, sub]
 
     wo_ring.last(keep_wo)
-    kv_ring.middle(n_chip - 3)
-    kv_ring.middle(n_chip - 2)
+    lax.fori_loop(n_chip - 4, n_chip - 1, lambda step, _: kv_ring.middle(step), None)
 
     def keep_kv(way, sub):
         out_rows = slice((2 * way + sub) * half_len, (2 * way + sub + 1) * half_len)
@@ -487,8 +519,6 @@
                 mate_copy(step, way, sub).wait_send()
 
     lax.fori_loop(0, n_chip, mates_sent, None)
-    for swap in swaps:
-        swap.wait_send()
 
 
 def finish_kernel(n_dev, h_ref, z_ref, wo_part_ref, a_ref, x_ref, dy_ref, gain_ref, wq_ref, wo_ref, wk_ref, wv_ref,
@@ -522,7 +552,7 @@
         pltpu.make_async_copy(h_ref, h_scr.at[mine], load_sems.at[0]),
         pltpu.make_async_copy(z_ref.at[:, cols(core, core_width)], z_scr.at[mine], load_sems.at[1]),
         pltpu.make_async_copy(z_ref, zf_scr, load_sems.at[2]),
-        pltpu.make_async_copy(a_ref, a_scr, load_sems.at[3]),
+        pltpu.make_async_copy(a_ref.at[mine], a_scr, load_sems.at[3]),
         pltpu.make_async_copy(x_ref, x_scr, load_sems.at[4]),
         pltpu.make_async_copy(dy_ref, dy_scr, load_sems.at[5]),
     ]
@@ -726,17 +756,17 @@
         )(x_flat, gain_row, w_key, w_value, cos_t, sin_t)
 
         groups = (n_groups, rows, head_dim)
-        kv_all, q_rows, da_rows, attn_flat, lse, delta = pl.pallas_call(
+        kv_all, q_rows, da_rows, attn_chip, dy_chip, lse, delta = pl.pallas_call(
             functools.partial(forward_kernel, n_dev),
             in_specs=[vmem, vmem, vmem, hbm, hbm, hbm, hbm],
-            out_specs=[hbm, hbm, hbm, hbm, vmem, vmem],
-            out_shape=(shape(n_seq, seq_len, kv_width), shape(*groups), shape(*groups), shape(n_rows, q_width),
+            out_specs=[hbm, hbm, hbm, hbm, hbm, vmem, vmem],
+            out_shape=(shape(n_seq, seq_len, kv_width), shape(*groups), shape(*groups), shape(2 * n_rows, q_width), shape(2 * n_rows, model_dim // 2),
                        shape(n_groups, 1, rows, dtype=f32), shape(n_groups, 1, rows, dtype=f32)),
             scratch_shapes=[pltpu.VMEM((n_rows, model_dim), bf16), pltpu.VMEM((n_rows, model_dim), bf16), pltpu.VMEM((n_seq, seq_len, kv_width), bf16),
                             pltpu.VMEM(groups, bf16), pltpu.VMEM(groups, bf16), pltpu.VMEM((n_groups, head_dim, rows), bf16), pltpu.VMEM((n_rows, q_width), bf16),
                             pltpu.VMEM((n_groups, head_dim, rows), f32), pltpu.VMEM((n_groups, 1, rows), f32), pltpu.VMEM((n_groups, 1, rows), f32),
                             pltpu.VMEM((2, model_dim, head_dim), bf16), pltpu.VMEM((2, head_dim, model_dim), bf16),
-                            dma((2,)), dma((3 + n_groups,)), dma((2, 2))] + gather_sems(),
+                            dma((3,)), dma((3 + n_groups,)), dma((2, 2)), dma((n_groups + 1,)), dma((n_groups + 1,))] + gather_sems(),
             compiler_params=comm(0), name='forward',
         )(kv_flat, cos_t, sin_t, h_flat, dy_flat, w_query, w_out)
 
@@ -753,10 +783,10 @@
                             pltpu.VMEM((2, 2, half_len, kv_width), f32), pltpu.VMEM((2, n_chip - 1, 2, half_len, kv_width), f32),
                             pltpu.VMEM((2 * n_rows, q_width), bf16), pltpu.VMEM((2 * n_rows, wo_cols), bf16),
                             pltpu.VMEM((2, n_sub, wo_sub, wo_cols), f32), pltpu.VMEM((2, n_chip - 1, n_sub, wo_sub, wo_cols), f32),
-                            dma((5,)), dma((2,)), dma((2,)), dma((2, 2)), dma((2, n_chip - 1, 2)), dma((2, n_chip, 2)), dma((2, n_chip, 2)),
+                            dma((5,)), dma((2, 2)), dma((2, n_chip - 1, 2)), dma((2, n_chip, 2)), dma((2, n_chip, 2)),
                             dma((2, n_sub)), dma((2, n_chip - 1, n_sub))],
             compiler_params=comm(1), name='attend_grad',
-        )(q_rows, kv_all, da_rows, lse, delta, cos_t, sin_t, attn_flat, dy_flat)
+        )(q_rows, kv_all, da_rows, lse, delta, cos_t, sin_t, attn_chip, dy_chip)
 
         core_width, sub_len = z_width // 2, model_dim // (2 * n_chip * n_sub)
         blk = model_dim // n_chip
@@ -774,7 +804,7 @@
                             dma((6,)), dma((2, 2)), dma((2,)), dma((2,)), dma((2, n_sub)), dma((2, n_chip - 1, n_sub))]
             + gather_sems() + gather_sems() + [dma((2, 2, n_sub)), dma((n_dev,)), dma((n_dev,))],
             compiler_params=comm(2), name='finish',
-        )(h_flat, z_flat, wo_part, attn_flat, x_flat, dy_flat, gain_row, w_query, w_out, w_key, w_value)
+        )(h_flat, z_flat, wo_part, attn_chip, x_flat, dy_flat, gain_row, w_query, w_out, w_key, w_value)
         n_blk = n_dev
         grad_wq, grad_wk, grad_wv, grad_wo, out_y, grad_x = pl.pallas_call(
             deliver_kernel,

time: 535 us -> 533 us (level)
  no operation moved by 1% of the time
where the time goes in v4:
time: 533 us; the launch traced here: 532 us
  Pallas kernels  529 us (99%)
    pallas_call x1, Pallas kernels, local_fn(): pl.pallas_call(functools.partial(finish_kernel, n_dev), in_specs=[hbm] *...  290 us
    pallas_call x1, Pallas kernels, local_fn(): pl.pallas_call(functools.partial(attend_grad_kernel, n_dev), in_specs=[hb...  147 us
    pallas_call x1, Pallas kernels, local_fn(): pl.pallas_call(functools.partial(forward_kernel, n_dev), in_specs=[vmem,...  59.7 us
    pallas_call x1, Pallas kernels, local_fn(): pl.pallas_call(deliver_kernel, in_specs=[hbm] * 4, out_specs=[hbm] * 6, o...  27.5 us

profile of v4, /device:TPU:21, one launch (start us, length us, event | category | flops | bytes accessed | tf_op | source)
XLA Modules:
  0.0 532.3 jit_solution(8910746662813069747)
XLA Ops:
  0.6 0.7 convert_element_type.10
  1.3 0.1 convert_element_type.11
  1.4 1.5 multiply_sine_fusion
  2.9 4.6 norm_kv.1
  7.6 59.7 %forward.1 = (bf16[2,3072,512]{2,1,0:T(8,128)(2,1)}, bf16[4,768,256]{2,1,0:T(8,128)(2,1)}, bf16[4,768,256]{2,1,0:T(8,128)(2,1)}, bf16[768,2048]{1,0:T(8,128)(2,1...) custom-call(bf16[384,512]{1,0:T(8,128)(2,1)} %get-tuple-element.30.kv_ref, ...), custom_call_target="tpu_custom_call" | custom-call | tf_op jit(solution)/shard_map/forward/pallas_call | solution.py:759
  67.2 146.8 %attend_grad.1 = (bf16[384,2560]{1,0:T(8,128)(2,1)}, f32[2,2,64,1024]{3,2,1,0:T(8,128)}) custom-call(bf16[4,768,256]{2,1,0:T(8,128)(2,1)} %get-tuple-element.31.q_ref, bf16[2,3072,512]{2,1,0:T(8,128)(2,1)} %get-tuple-element.32.kv_ref, bf16[4,768,256]{2,1,0:T(8,128)(2,1)} %get-tuple-element.33.da_ref, f32[4,1,768]{2,1,0:T(1,128)} %get-tuple-element.34.lse_ref, ...), custom_call_target="tpu_custom_call" | custom-call | tf_op jit(solution)/shard_map/attend_grad/pallas_call | solution.py:775
  214.1 290.0 %finish.1 = (f32[2048,2560]{1,0:T(8,128)}, f32[2048,2048]{1,0:T(8,128)}, bf16[384,2048]{1,0:T(8,128)(2,1)}, bf16[384,2048]{1,0:T(8,128)(2,1)}, f32[1,2048]{1,0:T(1,128)}) custom-call(bf16[384,2048]{1,0:T(8,128)(2,1)} %get-tuple-element.29.h_ref, bf16[384,2560]{1,0:T(8,128)(2,1)} %get-tuple-element.38.z_ref, ...), custom_call_target="tpu_custom_call" | custom-call | tf_op jit(solution)/shard_map/finish/pallas_call | solution.py:793
  504.1 0.0 copy-start
  504.1 27.5 %deliver.1 = (f32[2048,2048]{1,0:T(8,128)}, f32[2048,256]{1,0:T(8,128)}, f32[2048,256]{1,0:T(8,128)}, f32[2048,2048]{1,0:T(8,128)}, bf16[384,2048]{1,0:T(8,128)(2,1)}, /*index=5*/bf16[384,2048]{1,0:T(8,128)(2,1)}) custom-call(f32[2048,2560]{1,0:T(8,128)} %get-tuple-element.40.gz_ref, f32[2048,2048]{1,0:T(8,128)} %get-tuple-element.41.gwo_ref, ...), custom_call_target="tpu_custom_call" | custom-call | tf_op jit(solution)/shard_map/deliver/pallas_call | solution.py:809
  531.6 0.0 copy-done
  531.7 0.6 copy.16
  (1 shorter events, 0.0 us)
Async XLA Ops:
  504.1 27.6 %copy-start = (f32[1,2048]{1,0:T(1,128)S(1)}, f32[1,2048]{1,0:T(1,128)}, u32[]{:S(2)}) copy-start(f32[1,2048]{1,0:T(1,128)} %get-tuple-element.50) | copy-start | bytes 24580

commit v5 on v4

--- a/solution.py
+++ b/solution.py
@@ -166,6 +166,18 @@
     def last(self):
         self.middle(self.n_chip - 1, True)
 
+    def serve(self, step, sub):
+        for way in range(2):
+            self.onward(step - 1, way, sub).wait_recv()
+            self.onward(step - 1, way, sub).wait_send()
+
+            @pl.when(step < self.n_chip - 1)
+            def _():
+                self.onward(step, way, sub).start()
+
+            self.across(step - 1, way, sub).wait_send()
+            self.across(step, way, sub).start()
+
     def drain(self):
         for sub, way in self.each:
             self.across(self.n_chip - 1, way, sub).wait_send()
@@ -243,22 +255,20 @@
     dy_swap.start()
 
     def project(head, slot):
-        @pl.when(head < num_heads)
-        def _():
-            for copy in weights(head, slot):
-                copy.wait()
-
-            @pl.when(head + 1 < num_heads)
-            def _():
-                for copy in weights(head + 1, 1 - slot):
-                    copy.start()
-
-            head_rows = pl.ds(pl.multiple_of(head * half_len, half_len), half_len)
-            q_new = rotate(dot(h_scr[...], wq_buf[slot], NN), cos_ref[...], sin_ref[...]).astype(jnp.bfloat16)
-            da_new = dot(dy_scr[...], wo_buf[slot], NT).astype(jnp.bfloat16)
-            for group in range(n_groups):
-                q_scr[group, head_rows, :] = q_new[group * half_len:(group + 1) * half_len, :]
-                da_scr[group, head_rows, :] = da_new[group * half_len:(group + 1) * half_len, :]
+        for copy in weights(head, slot):
+            copy.wait()
+
+        @pl.when(head + 1 < num_heads)
+        def _():
+            for copy in weights(head + 1, 1 - slot):
+                copy.start()
+
+        head_rows = pl.ds(pl.multiple_of(head * half_len, half_len), half_len)
+        q_new = rotate(dot(h_scr[...], wq_buf[slot], NN), cos_ref[...], sin_ref[...]).astype(jnp.bfloat16)
+        da_new = dot(dy_scr[...], wo_buf[slot], NT).astype(jnp.bfloat16)
+        for group in range(n_groups):
+            q_scr[group, head_rows, :] = q_new[group * half_len:(group + 1) * half_len, :]
+            da_scr[group, head_rows, :] = da_new[group * half_len:(group + 1) * half_len, :]
 
     def block(seq, group, start, key_len, masked):
         index = 2 * seq + group
@@ -308,37 +318,32 @@
         def _():
             block(seq, 1, (n_dev - 1 - back) * chip_len, chip_len, True)
 
-    def project_two(step):
-        lax.fori_loop(2 * step, 2 * step + 2, lambda head, _: project(head, lax.rem(head, 2)), None)
-
-    project_two(0)
-    ring.middle(1)
-
-    def projecting(step, _):
-        project_two(step)
-        ring.middle(step + 1)
-
-    lax.fori_loop(1, 3, projecting, None)
-    lax.fori_loop(6, max(num_heads, 6), lambda head, _: project(head, lax.rem(head, 2)), None)
-    for group in range(n_groups):
-        qt_scr[group] = q_scr[group].T
-    ring.middle(4)
     saves = [pltpu.make_async_copy(q_scr, q_ref, out_sems.at[0]), pltpu.make_async_copy(da_scr, da_ref, out_sems.at[1])]
-    for save in saves:
-        save.start()
-
-    def attend(turn, _):
+
+    def attend(turn):
         attend_pair(lax.div(turn, n_seq), lax.rem(turn, n_seq))
 
-        @pl.when(turn < n_chip - 6)
-        def _():
-            ring.middle(turn + 5)
-
-        @pl.when(turn == n_chip - 6)
-        def _():
-            ring.last()
-
-    lax.fori_loop(0, n_chip // 2 * n_seq, attend, None)
+    def work(turn, _):
+        @pl.when(turn < num_heads)
+        def _():
+            project(turn, lax.rem(turn, 2))
+
+        @pl.when(turn == n_chip - 1)
+        def _():
+            for group in range(n_groups):
+                qt_scr[group] = q_scr[group].T
+            for save in saves:
+                save.start()
+
+        @pl.when(turn >= n_chip)
+        def _():
+            attend(turn - n_chip)
+
+        @pl.when(turn < n_seq * (n_chip - 1))
+        def _():
+            ring.serve(lax.div(turn, n_seq) + 1, lax.rem(turn, n_seq))
+
+    lax.fori_loop(0, n_chip + n_chip // 2 * n_seq, work, None)
     for sub, way in ring.each:
         ring.across(n_chip - 1, way, sub).wait_send()
     saves.append(pltpu.make_async_copy(kv_scr, all_ref, out_sems.at[2]))

time: 533 us -> 528 us (level)
    pallas_call x1, Pallas kernels: 59.7 us -> 54.2 us  [local_fn(): pl.pallas_call(functools.partial(forward_kernel, n_dev), in_specs=[vmem,...]
where the time goes in v5:
time: 528 us; the launch traced here: 527 us
  Pallas kernels  524 us (99%)
    pallas_call x1, Pallas kernels, local_fn(): pl.pallas_call(functools.partial(finish_kernel, n_dev), in_specs=[hbm] *...  291 us
    pallas_call x1, Pallas kernels, local_fn(): pl.pallas_call(functools.partial(attend_grad_kernel, n_dev), in_specs=[hb...  147 us
    pallas_call x1, Pallas kernels, local_fn(): pl.pallas_call(functools.partial(forward_kernel, n_dev), in_specs=[vmem,...  54.2 us
    pallas_call x1, Pallas kernels, local_fn(): pl.pallas_call(deliver_kernel, in_specs=[hbm] * 4, out_specs=[hbm] * 6, o...  27.5 us

profile of v5, /device:TPU:21, one launch (start us, length us, event | category | flops | bytes accessed | tf_op | source)
XLA Modules:
  0.0 527.5 jit_solution(2464732955618791558)
XLA Ops:
  0.6 0.7 convert_element_type.10
  1.3 0.1 convert_element_type.11
  1.4 1.5 multiply_sine_fusion
  2.9 4.6 norm_kv.1
  7.6 54.2 %forward.1 = (bf16[2,3072,512]{2,1,0:T(8,128)(2,1)}, bf16[4,768,256]{2,1,0:T(8,128)(2,1)}, bf16[4,768,256]{2,1,0:T(8,128)(2,1)}, bf16[768,2048]{1,0:T(8,128)(2,1...) custom-call(bf16[384,512]{1,0:T(8,128)(2,1)} %get-tuple-element.30.kv_ref, ...), custom_call_target="tpu_custom_call" | custom-call | tf_op jit(solution)/shard_map/forward/pallas_call | solution.py:764
  61.7 146.9 %attend_grad.1 = (bf16[384,2560]{1,0:T(8,128)(2,1)}, f32[2,2,64,1024]{3,2,1,0:T(8,128)}) custom-call(bf16[4,768,256]{2,1,0:T(8,128)(2,1)} %get-tuple-element.31.q_ref, bf16[2,3072,512]{2,1,0:T(8,128)(2,1)} %get-tuple-element.32.kv_ref, bf16[4,768,256]{2,1,0:T(8,128)(2,1)} %get-tuple-element.33.da_ref, f32[4,1,768]{2,1,0:T(1,128)} %get-tuple-element.34.lse_ref, ...), custom_call_target="tpu_custom_call" | custom-call | tf_op jit(solution)/shard_map/attend_grad/pallas_call | solution.py:780
  208.6 290.7 %finish.1 = (f32[2048,2560]{1,0:T(8,128)}, f32[2048,2048]{1,0:T(8,128)}, bf16[384,2048]{1,0:T(8,128)(2,1)}, bf16[384,2048]{1,0:T(8,128)(2,1)}, f32[1,2048]{1,0:T(1,128)}) custom-call(bf16[384,2048]{1,0:T(8,128)(2,1)} %get-tuple-element.29.h_ref, bf16[384,2560]{1,0:T(8,128)(2,1)} %get-tuple-element.38.z_ref, ...), custom_call_target="tpu_custom_call" | custom-call | tf_op jit(solution)/shard_map/finish/pallas_call | solution.py:798
  499.3 0.0 copy-start
  499.3 27.5 %deliver.1 = (f32[2048,2048]{1,0:T(8,128)}, f32[2048,256]{1,0:T(8,128)}, f32[2048,256]{1,0:T(8,128)}, f32[2048,2048]{1,0:T(8,128)}, bf16[384,2048]{1,0:T(8,128)(2,1)}, /*index=5*/bf16[384,2048]{1,0:T(8,128)(2,1)}) custom-call(f32[2048,2560]{1,0:T(8,128)} %get-tuple-element.40.gz_ref, f32[2048,2048]{1,0:T(8,128)} %get-tuple-element.41.gwo_ref, ...), custom_call_target="tpu_custom_call" | custom-call | tf_op jit(solution)/shard_map/deliver/pallas_call | solution.py:814
  526.9 0.0 copy-done
  526.9 0.6 copy.16
  (1 shorter events, 0.0 us)
Async XLA Ops:
  499.3 27.6 %copy-start = (f32[1,2048]{1,0:T(1,128)S(1)}, f32[1,2048]{1,0:T(1,128)}, u32[]{:S(2)}) copy-start(f32[1,2048]{1,0:T(1,128)} %get-tuple-element.50) | copy-start | bytes 24580
